TPU v7x, 16 devices: a whole 2x2x2 slice. The times are simulated.
16 devices in a mesh: dp: 1, tp: 16 (over x, y, z, core).
Axes of the slice: x: 2, y: 2, z: 2, core: 2. Of those that a mesh axis runs over, the one named last changes fastest.
Arguments:
- x: bfloat16 [5120, 3584], P(('dp', 'tp'))
- dy: bfloat16 [5120, 3584], P(('dp', 'tp'))
- gate: bfloat16 [5120, 14336], P('dp', 'tp')
- up: bfloat16 [5120, 14336], P('dp', 'tp')
- w_gate: bfloat16 [3584, 14336], P(None, 'tp')
- w_up: bfloat16 [3584, 14336], P(None, 'tp')
- w_down: bfloat16 [14336, 3584], P('tp')
Outputs:
- output 1: bfloat16 [5120, 3584], P(('dp', 'tp'))
- output 2: bfloat16 [3584, 14336], P('dp', 'tp')
- output 3: bfloat16 [3584, 14336], P('dp', 'tp')
- output 4: bfloat16 [14336, 3584], P(('dp', 'tp'))
All inputs are finite; a program needn't handle non-finite values.
Results may differ from a plain program's by a relative error of at most 0.012.
Values are sent between devices in bfloat16 or wider.
A program may use at most 2 GiB of HBM per device.

v0:
```python
import jax
import jax.numpy as jnp


def act(gate, up):
    return jax.nn.gelu(gate) * up


def solution(mesh):
    def step(x, dy, gate, up, w_gate, w_up, w_down):
        hidden, back = jax.vjp(act, gate.astype(jnp.float32), up.astype(jnp.float32))
        d_hidden = jnp.dot(dy, w_down.T, preferred_element_type=jnp.float32)
        d_gate, d_up = (g.astype(jnp.bfloat16) for g in back(d_hidden))
        dx = jnp.dot(d_gate, w_gate.T) + jnp.dot(d_up, w_up.T)
        groups = mesh.shape["dp"]

        def by_group(a, b):
            a, b = (t.reshape(groups, -1, t.shape[-1]) for t in (a, b))
            product = jnp.einsum("gta,gtb->gab", a, b, preferred_element_type=jnp.float32)
            return product.astype(jnp.bfloat16).reshape(-1, b.shape[-1])

        return dx, by_group(x, d_gate), by_group(x, d_up), by_group(hidden.astype(jnp.bfloat16), dy)

    return step
```

profile of v0, /device:TPU:0, one launch (start us, length us, event | category | flops | bytes accessed | tf_op | source)
XLA Modules:
  0.0 1407.0 jit_solution(17988947720283223197)
XLA Ops:
  8.7 145.9 %all-gather.7.cloned.1.call-done = bf16[5120,3584]{1,0:T(8,128)(2,1)} async-done(((bf16[320,3584]{1,0:T(8,128)(2,1)}), bf16[5120,3584]{1,0:T(8,128)(2,1)}) %all-gather.7.cloned.1.call-update) | async-done | bytes 36700176 | tf_op args[1]
  154.6 58.1 %fusion.36 = (bf16[5120,896]{1,0:T(8,128)(2,1)}, bf16[5120,896]{1,0:T(8,128)(2,1)}) fusion(bf16[5120,896]{1,0:T(8,128)(2,1)} %param.7, bf16[5120,896]{1,0:T(8,128)(2,1)} %param.6, bf16[5120,3584]{1,0:T(8,128)(2,1)} %all-gather.7.cloned.1.call-done, bf16[896,3584]{1,0:T(8,128)(2,1)} %param.5), kind=kOutput, calls=%fused_computation.59 | convolution fusion | flops 33002618880 | bytes 79822848 | tf_op jit(solution)/dot_general | solution.py:12
  212.8 526.6 %while.4 = (bf16[5120,896]{1,0:T(8,128)(2,1)}, bf16[3584,896]{1,0:T(8,128)(2,1)}, bf16[320,3584]{1,0:T(8,128)(2,1)}, bf16[320,3584]{1,0:T(8,128)(2,1)}, u32[]{:T...) while((bf16[5120,896]{1,0:T(8,128)(2,1)}, ...), condition=%wide.windowed_dot_general_cond_rs.clone, body=%wide.windowed_dot_general_body_rs.clone.sunk | while | flops 8232304640 | bytes 122946168 | solution.py:14
  227.7 22.0 %collective-permute-done = bf16[320,3584]{1,0:T(8,128)(2,1)} collective-permute-done((bf16[320,3584]{1,0:T(8,128)(2,1)}, bf16[320,3584]{1,0:T(8,128)(2,1)}, u32[]{:S(2)}, u32[]{:S(2)}) %collective-permute-start) | collective-permute-done | bytes 2293792 | tf_op jit(solution)/dot_general | solution.py:14
  254.8 77.1 %collective-permute-start.2 = (bf16[320,3584]{1,0:T(8,128)(2,1)}, bf16[320,3584]{1,0:T(8,128)(2,1)}, u32[]{:S(2)}, u32[]{:S(2)}) collective-permute-start(bf16[320,3584]{1,0:T(8,128)(2,1)} %get-tuple-element.151), channel_id=6, source_target_pairs={{0,1},{1,2},{2,3},{3,4},{4,5},{5,6},{6,7},{7,8},{8,9},{9,10},{10,1... | collective-permute-start | bytes 6881288 | tf_op jit(solution)/dot_general | solution.py:14
  366.1 54.1 %collective-permute-start = (bf16[320,3584]{1,0:T(8,128)(2,1)}, bf16[320,3584]{1,0:T(8,128)(2,1)}, u32[]{:S(2)}, u32[]{:S(2)}) collective-permute-start(bf16[320,3584]{1,0:T(8,128)(2,1)} %broadcast_select_fusion.8), channel_id=4, source_target_pairs={{0,1},{1,2},{2,3},{3,4},{4,5},{5,6},{6,7},{7,8},{8,9},{9,10},{10,1... | collective-permute-start | bytes 6881288 | tf_op jit(solution)/dot_general | solution.py:14
  452.6 22.4 %collective-permute-start.2 = (bf16[320,3584]{1,0:T(8,128)(2,1)}, bf16[320,3584]{1,0:T(8,128)(2,1)}, u32[]{:S(2)}, u32[]{:S(2)}) collective-permute-start(bf16[320,3584]{1,0:T(8,128)(2,1)} %get-tuple-element.151), channel_id=6, source_target_pairs={{0,1},{1,2},{2,3},{3,4},{4,5},{5,6},{6,7},{7,8},{8,9},{9,10},{10,1... | collective-permute-start | bytes 6881288 | tf_op jit(solution)/dot_general | solution.py:14
  509.0 25.2 %collective-permute-start = (bf16[320,3584]{1,0:T(8,128)(2,1)}, bf16[320,3584]{1,0:T(8,128)(2,1)}, u32[]{:S(2)}, u32[]{:S(2)}) collective-permute-start(bf16[320,3584]{1,0:T(8,128)(2,1)} %broadcast_select_fusion.8), channel_id=4, source_target_pairs={{0,1},{1,2},{2,3},{3,4},{4,5},{5,6},{6,7},{7,8},{8,9},{9,10},{10,1... | collective-permute-start | bytes 6881288 | tf_op jit(solution)/dot_general | solution.py:14
  566.6 24.9 %collective-permute-start.2 = (bf16[320,3584]{1,0:T(8,128)(2,1)}, bf16[320,3584]{1,0:T(8,128)(2,1)}, u32[]{:S(2)}, u32[]{:S(2)}) collective-permute-start(bf16[320,3584]{1,0:T(8,128)(2,1)} %get-tuple-element.151), channel_id=6, source_target_pairs={{0,1},{1,2},{2,3},{3,4},{4,5},{5,6},{6,7},{7,8},{8,9},{9,10},{10,1... | collective-permute-start | bytes 6881288 | tf_op jit(solution)/dot_general | solution.py:14
  625.6 25.8 %collective-permute-start = (bf16[320,3584]{1,0:T(8,128)(2,1)}, bf16[320,3584]{1,0:T(8,128)(2,1)}, u32[]{:S(2)}, u32[]{:S(2)}) collective-permute-start(bf16[320,3584]{1,0:T(8,128)(2,1)} %broadcast_select_fusion.8), channel_id=4, source_target_pairs={{0,1},{1,2},{2,3},{3,4},{4,5},{5,6},{6,7},{7,8},{8,9},{9,10},{10,1... | collective-permute-start | bytes 6881288 | tf_op jit(solution)/dot_general | solution.py:14
  683.7 24.9 %collective-permute-start.2 = (bf16[320,3584]{1,0:T(8,128)(2,1)}, bf16[320,3584]{1,0:T(8,128)(2,1)}, u32[]{:S(2)}, u32[]{:S(2)}) collective-permute-start(bf16[320,3584]{1,0:T(8,128)(2,1)} %get-tuple-element.151), channel_id=6, source_target_pairs={{0,1},{1,2},{2,3},{3,4},{4,5},{5,6},{6,7},{7,8},{8,9},{9,10},{10,1... | collective-permute-start | bytes 6881288 | tf_op jit(solution)/dot_general | solution.py:14
  739.3 25.2 %collective-permute-start.8 = (bf16[320,3584]{1,0:T(8,128)(2,1)}, bf16[320,3584]{1,0:T(8,128)(2,1)}, u32[]{:S(2)}, u32[]{:S(2)}) collective-permute-start(bf16[320,3584]{1,0:T(8,128)(2,1)} %get-tuple-element.13), channel_id=7, source_target_pairs={{0,1},{1,2},{2,3},{3,4},{4,5},{5,6},{6,7},{7,8},{8,9},{9,10},{10,1... | collective-permute-start | bytes 6881288 | tf_op jit(solution)/dot_general | solution.py:14
  764.5 457.5 %while.5 = (bf16[5120,896]{1,0:T(8,128)(2,1)}, bf16[3584,896]{1,0:T(8,128)(2,1)}, bf16[320,3584]{1,0:T(8,128)(2,1)S(1)}, bf16[320,3584]{1,0:T(8,128)(2,1)}, u32[...) while((bf16[5120,896]{1,0:T(8,128)(2,1)}, ...), condition=%wide.windowed_dot_general_cond_rs.1.clone, body=%wide.windowed_dot_general_body_rs.1.clone.sunk | while | flops 8232304640 | bytes 113771096 | solution.py:14
  801.4 47.5 %collective-permute-start.6 = (bf16[320,3584]{1,0:T(8,128)(2,1)}, bf16[320,3584]{1,0:T(8,128)(2,1)}, u32[]{:S(2)}, u32[]{:S(2)}) collective-permute-start(bf16[320,3584]{1,0:T(8,128)(2,1)} %get-tuple-element.160), channel_id=12, source_target_pairs={{0,1},{1,2},{2,3},{3,4},{4,5},{5,6},{6,7},{7,8},{8,9},{9,10},{10,1... | collective-permute-start | bytes 6881288 | tf_op jit(solution)/dot_general | solution.py:14
  882.2 23.9 %collective-permute-start.4 = (bf16[320,3584]{1,0:T(8,128)(2,1)}, bf16[320,3584]{1,0:T(8,128)(2,1)}, u32[]{:S(2)}, u32[]{:S(2)}) collective-permute-start(bf16[320,3584]{1,0:T(8,128)(2,1)} %broadcast_select_fusion.10), channel_id=10, source_target_pairs={{0,1},{1,2},{2,3},{3,4},{4,5},{5,6},{6,7},{7,8},{8,9},{9,10},{10,1... | collective-permute-start | bytes 6881288 | tf_op jit(solution)/dot_general | solution.py:14
  937.6 24.0 %collective-permute-start.6 = (bf16[320,3584]{1,0:T(8,128)(2,1)}, bf16[320,3584]{1,0:T(8,128)(2,1)}, u32[]{:S(2)}, u32[]{:S(2)}) collective-permute-start(bf16[320,3584]{1,0:T(8,128)(2,1)} %get-tuple-element.160), channel_id=12, source_target_pairs={{0,1},{1,2},{2,3},{3,4},{4,5},{5,6},{6,7},{7,8},{8,9},{9,10},{10,1... | collective-permute-start | bytes 6881288 | tf_op jit(solution)/dot_general | solution.py:14
  994.9 24.9 %collective-permute-start.4 = (bf16[320,3584]{1,0:T(8,128)(2,1)}, bf16[320,3584]{1,0:T(8,128)(2,1)}, u32[]{:S(2)}, u32[]{:S(2)}) collective-permute-start(bf16[320,3584]{1,0:T(8,128)(2,1)} %broadcast_select_fusion.10), channel_id=10, source_target_pairs={{0,1},{1,2},{2,3},{3,4},{4,5},{5,6},{6,7},{7,8},{8,9},{9,10},{10,1... | collective-permute-start | bytes 6881288 | tf_op jit(solution)/dot_general | solution.py:14
  1051.3 24.9 %collective-permute-start.6 = (bf16[320,3584]{1,0:T(8,128)(2,1)}, bf16[320,3584]{1,0:T(8,128)(2,1)}, u32[]{:S(2)}, u32[]{:S(2)}) collective-permute-start(bf16[320,3584]{1,0:T(8,128)(2,1)} %get-tuple-element.160), channel_id=12, source_target_pairs={{0,1},{1,2},{2,3},{3,4},{4,5},{5,6},{6,7},{7,8},{8,9},{9,10},{10,1... | collective-permute-start | bytes 6881288 | tf_op jit(solution)/dot_general | solution.py:14
  1109.5 26.1 %collective-permute-start.4 = (bf16[320,3584]{1,0:T(8,128)(2,1)}, bf16[320,3584]{1,0:T(8,128)(2,1)}, u32[]{:S(2)}, u32[]{:S(2)}) collective-permute-start(bf16[320,3584]{1,0:T(8,128)(2,1)} %broadcast_select_fusion.10), channel_id=10, source_target_pairs={{0,1},{1,2},{2,3},{3,4},{4,5},{5,6},{6,7},{7,8},{8,9},{9,10},{10,1... | collective-permute-start | bytes 6881288 | tf_op jit(solution)/dot_general | solution.py:14
  1167.1 24.9 %collective-permute-start.6 = (bf16[320,3584]{1,0:T(8,128)(2,1)}, bf16[320,3584]{1,0:T(8,128)(2,1)}, u32[]{:S(2)}, u32[]{:S(2)}) collective-permute-start(bf16[320,3584]{1,0:T(8,128)(2,1)} %get-tuple-element.160), channel_id=12, source_target_pairs={{0,1},{1,2},{2,3},{3,4},{4,5},{5,6},{6,7},{7,8},{8,9},{9,10},{10,1... | collective-permute-start | bytes 6881288 | tf_op jit(solution)/dot_general | solution.py:14
  1222.0 24.9 %collective-permute-start.9 = (bf16[320,3584]{1,0:T(8,128)(2,1)}, bf16[320,3584]{1,0:T(8,128)(2,1)}, u32[]{:S(2)}, u32[]{:S(2)}) collective-permute-start(bf16[320,3584]{1,0:T(8,128)(2,1)} %get-tuple-element.15), channel_id=13, source_target_pairs={{0,1},{1,2},{2,3},{3,4},{4,5},{5,6},{6,7},{7,8},{8,9},{9,10},{10,1... | collective-permute-start | bytes 6881288 | tf_op jit(solution)/dot_general | solution.py:14
  1247.0 40.6 %fusion.51 = bf16[3584,896]{0,1:T(8,128)(2,1)} fusion(bf16[5120,896]{1,0:T(8,128)(2,1)} %get-tuple-element.248, bf16[5120,3584]{1,0:T(8,128)(2,1)} %all-gather.9.cloned.1.call-done), kind=kOutput, calls=%fused_computation.74 | convolution fusion | flops 32886554624 | bytes 52297728 | tf_op jit(solution)/gta,gtb->gab/dot_general | solution.py:19
  1297.2 40.9 %fusion.52 = bf16[3584,896]{0,1:T(8,128)(2,1)} fusion(bf16[5120,896]{1,0:T(8,128)(2,1)} %get-tuple-element.247, bf16[5120,3584]{1,0:T(8,128)(2,1)} %all-gather.9.cloned.1.call-done), kind=kOutput, calls=%fused_computation.75 | convolution fusion | flops 32886554624 | bytes 52297728 | tf_op jit(solution)/gta,gtb->gab/dot_general | solution.py:19
  1347.6 47.9 %fusion.48 = bf16[896,3584]{1,0:T(8,128)(2,1)} fusion(bf16[5120,3584]{1,0:T(8,128)(2,1)} %all-gather.7.cloned.1.call-done, bf16[5120,896]{1,0:T(8,128)(2,1)} %param.6, bf16[5120,896]{1,0:T(8,128)(2,1)} %param.7), kind=kOutput, calls=%fused_computation.71 | convolution fusion | flops 32941604864 | bytes 61472768 | tf_op jit(solution)/gta,gtb->gab/dot_general | solution.py:19
  (123 shorter events, 535.7 us)
Async XLA Ops:
  7.2 147.5 %all-gather.7.cloned.1.call-start = ((), (), s32[]{:S(2)}) async-start(), calls=%async_computation | async-start | bytes 38993920 | tf_op args[1]
  7.9 1239.1 %all-gather.9.cloned.1.call-start = ((), (), s32[]{:S(2)}) async-start(), calls=%async_computation.1 | async-start | bytes 38993920 | tf_op args[0]
  214.5 35.2 %collective-permute-start = (bf16[320,3584]{1,0:T(8,128)(2,1)}, bf16[320,3584]{1,0:T(8,128)(2,1)}, u32[]{:S(2)}, u32[]{:S(2)}) collective-permute-start(bf16[320,3584]{1,0:T(8,128)(2,1)} %broadcast_select_fusion.8), channel_id=4, source_target_pairs={{0,1},{1,2},{2,3},{3,4},{4,5},{5,6},{6,7},{7,8},{8,9},{9,10},{10,1... | collective-permute-start | bytes 6881288 | tf_op jit(solution)/dot_general | solution.py:14
  217.1 32.6 %collective-permute-start.1 = (bf16[320,3584]{1,0:T(8,128)(2,1)}, bf16[320,3584]{1,0:T(8,128)(2,1)}, u32[]{:S(2)}, u32[]{:S(2)}) collective-permute-start(bf16[320,3584]{1,0:T(8,128)(2,1)} %broadcast_select_fusion.9), channel_id=3, source_target_pairs={{0,15},{1,0},{2,1},{3,2},{4,3},{5,4},{6,5},{7,6},{8,7},{9,8},{10,9... | collective-permute-start | bytes 6881288 | tf_op jit(solution)/dot_general | solution.py:14
  254.8 85.2 %collective-permute-start.2 = (bf16[320,3584]{1,0:T(8,128)(2,1)}, bf16[320,3584]{1,0:T(8,128)(2,1)}, u32[]{:S(2)}, u32[]{:S(2)}) collective-permute-start(bf16[320,3584]{1,0:T(8,128)(2,1)} %get-tuple-element.151), channel_id=6, source_target_pairs={{0,1},{1,2},{2,3},{3,4},{4,5},{5,6},{6,7},{7,8},{8,9},{9,10},{10,1... | collective-permute-start | bytes 6881288 | tf_op jit(solution)/dot_general | solution.py:14
  331.8 25.9 %collective-permute-start.3 = (bf16[320,3584]{1,0:T(8,128)(2,1)}, bf16[320,3584]{1,0:T(8,128)(2,1)}, u32[]{:S(2)}, u32[]{:S(2)}) collective-permute-start(bf16[320,3584]{1,0:T(8,128)(2,1)} %get-tuple-element.152), channel_id=5, source_target_pairs={{0,15},{1,0},{2,1},{3,2},{4,3},{5,4},{6,5},{7,6},{8,7},{9,8},{10,9... | collective-permute-start | bytes 6881288 | tf_op jit(solution)/dot_general | solution.py:14
  366.1 63.8 %collective-permute-start = (bf16[320,3584]{1,0:T(8,128)(2,1)}, bf16[320,3584]{1,0:T(8,128)(2,1)}, u32[]{:S(2)}, u32[]{:S(2)}) collective-permute-start(bf16[320,3584]{1,0:T(8,128)(2,1)} %broadcast_select_fusion.8), channel_id=4, source_target_pairs={{0,1},{1,2},{2,3},{3,4},{4,5},{5,6},{6,7},{7,8},{8,9},{9,10},{10,1... | collective-permute-start | bytes 6881288 | tf_op jit(solution)/dot_general | solution.py:14
  452.6 30.5 %collective-permute-start.2 = (bf16[320,3584]{1,0:T(8,128)(2,1)}, bf16[320,3584]{1,0:T(8,128)(2,1)}, u32[]{:S(2)}, u32[]{:S(2)}) collective-permute-start(bf16[320,3584]{1,0:T(8,128)(2,1)} %get-tuple-element.151), channel_id=6, source_target_pairs={{0,1},{1,2},{2,3},{3,4},{4,5},{5,6},{6,7},{7,8},{8,9},{9,10},{10,1... | collective-permute-start | bytes 6881288 | tf_op jit(solution)/dot_general | solution.py:14
  509.0 34.9 %collective-permute-start = (bf16[320,3584]{1,0:T(8,128)(2,1)}, bf16[320,3584]{1,0:T(8,128)(2,1)}, u32[]{:S(2)}, u32[]{:S(2)}) collective-permute-start(bf16[320,3584]{1,0:T(8,128)(2,1)} %broadcast_select_fusion.8), channel_id=4, source_target_pairs={{0,1},{1,2},{2,3},{3,4},{4,5},{5,6},{6,7},{7,8},{8,9},{9,10},{10,1... | collective-permute-start | bytes 6881288 | tf_op jit(solution)/dot_general | solution.py:14
  566.6 33.0 %collective-permute-start.2 = (bf16[320,3584]{1,0:T(8,128)(2,1)}, bf16[320,3584]{1,0:T(8,128)(2,1)}, u32[]{:S(2)}, u32[]{:S(2)}) collective-permute-start(bf16[320,3584]{1,0:T(8,128)(2,1)} %get-tuple-element.151), channel_id=6, source_target_pairs={{0,1},{1,2},{2,3},{3,4},{4,5},{5,6},{6,7},{7,8},{8,9},{9,10},{10,1... | collective-permute-start | bytes 6881288 | tf_op jit(solution)/dot_general | solution.py:14
  625.6 35.5 %collective-permute-start = (bf16[320,3584]{1,0:T(8,128)(2,1)}, bf16[320,3584]{1,0:T(8,128)(2,1)}, u32[]{:S(2)}, u32[]{:S(2)}) collective-permute-start(bf16[320,3584]{1,0:T(8,128)(2,1)} %broadcast_select_fusion.8), channel_id=4, source_target_pairs={{0,1},{1,2},{2,3},{3,4},{4,5},{5,6},{6,7},{7,8},{8,9},{9,10},{10,1... | collective-permute-start | bytes 6881288 | tf_op jit(solution)/dot_general | solution.py:14
  683.7 33.0 %collective-permute-start.2 = (bf16[320,3584]{1,0:T(8,128)(2,1)}, bf16[320,3584]{1,0:T(8,128)(2,1)}, u32[]{:S(2)}, u32[]{:S(2)}) collective-permute-start(bf16[320,3584]{1,0:T(8,128)(2,1)} %get-tuple-element.151), channel_id=6, source_target_pairs={{0,1},{1,2},{2,3},{3,4},{4,5},{5,6},{6,7},{7,8},{8,9},{9,10},{10,1... | collective-permute-start | bytes 6881288 | tf_op jit(solution)/dot_general | solution.py:14
  739.3 656.1 %collective-permute-start.8 = (bf16[320,3584]{1,0:T(8,128)(2,1)}, bf16[320,3584]{1,0:T(8,128)(2,1)}, u32[]{:S(2)}, u32[]{:S(2)}) collective-permute-start(bf16[320,3584]{1,0:T(8,128)(2,1)} %get-tuple-element.13), channel_id=7, source_target_pairs={{0,1},{1,2},{2,3},{3,4},{4,5},{5,6},{6,7},{7,8},{8,9},{9,10},{10,1... | collective-permute-start | bytes 6881288 | tf_op jit(solution)/dot_general | solution.py:14
  766.3 29.4 %collective-permute-start.4 = (bf16[320,3584]{1,0:T(8,128)(2,1)}, bf16[320,3584]{1,0:T(8,128)(2,1)}, u32[]{:S(2)}, u32[]{:S(2)}) collective-permute-start(bf16[320,3584]{1,0:T(8,128)(2,1)} %broadcast_select_fusion.10), channel_id=10, source_target_pairs={{0,1},{1,2},{2,3},{3,4},{4,5},{5,6},{6,7},{7,8},{8,9},{9,10},{10,1... | collective-permute-start | bytes 6881288 | tf_op jit(solution)/dot_general | solution.py:14
  770.3 26.8 %collective-permute-start.5 = (bf16[320,3584]{1,0:T(8,128)(2,1)}, bf16[320,3584]{1,0:T(8,128)(2,1)}, u32[]{:S(2)}, u32[]{:S(2)}) collective-permute-start(bf16[320,3584]{1,0:T(8,128)(2,1)} %broadcast_select_fusion.11), channel_id=9, source_target_pairs={{0,15},{1,0},{2,1},{3,2},{4,3},{5,4},{6,5},{7,6},{8,7},{9,8},{10,9... | collective-permute-start | bytes 6881288 | tf_op jit(solution)/dot_general | solution.py:14
  801.4 55.7 %collective-permute-start.6 = (bf16[320,3584]{1,0:T(8,128)(2,1)}, bf16[320,3584]{1,0:T(8,128)(2,1)}, u32[]{:S(2)}, u32[]{:S(2)}) collective-permute-start(bf16[320,3584]{1,0:T(8,128)(2,1)} %get-tuple-element.160), channel_id=12, source_target_pairs={{0,1},{1,2},{2,3},{3,4},{4,5},{5,6},{6,7},{7,8},{8,9},{9,10},{10,1... | collective-permute-start | bytes 6881288 | tf_op jit(solution)/dot_general | solution.py:14
  882.2 33.6 %collective-permute-start.4 = (bf16[320,3584]{1,0:T(8,128)(2,1)}, bf16[320,3584]{1,0:T(8,128)(2,1)}, u32[]{:S(2)}, u32[]{:S(2)}) collective-permute-start(bf16[320,3584]{1,0:T(8,128)(2,1)} %broadcast_select_fusion.10), channel_id=10, source_target_pairs={{0,1},{1,2},{2,3},{3,4},{4,5},{5,6},{6,7},{7,8},{8,9},{9,10},{10,1... | collective-permute-start | bytes 6881288 | tf_op jit(solution)/dot_general | solution.py:14
  937.6 32.2 %collective-permute-start.6 = (bf16[320,3584]{1,0:T(8,128)(2,1)}, bf16[320,3584]{1,0:T(8,128)(2,1)}, u32[]{:S(2)}, u32[]{:S(2)}) collective-permute-start(bf16[320,3584]{1,0:T(8,128)(2,1)} %get-tuple-element.160), channel_id=12, source_target_pairs={{0,1},{1,2},{2,3},{3,4},{4,5},{5,6},{6,7},{7,8},{8,9},{9,10},{10,1... | collective-permute-start | bytes 6881288 | tf_op jit(solution)/dot_general | solution.py:14
  994.9 34.6 %collective-permute-start.4 = (bf16[320,3584]{1,0:T(8,128)(2,1)}, bf16[320,3584]{1,0:T(8,128)(2,1)}, u32[]{:S(2)}, u32[]{:S(2)}) collective-permute-start(bf16[320,3584]{1,0:T(8,128)(2,1)} %broadcast_select_fusion.10), channel_id=10, source_target_pairs={{0,1},{1,2},{2,3},{3,4},{4,5},{5,6},{6,7},{7,8},{8,9},{9,10},{10,1... | collective-permute-start | bytes 6881288 | tf_op jit(solution)/dot_general | solution.py:14
  1021.3 25.7 %collective-permute-start.5 = (bf16[320,3584]{1,0:T(8,128)(2,1)}, bf16[320,3584]{1,0:T(8,128)(2,1)}, u32[]{:S(2)}, u32[]{:S(2)}) collective-permute-start(bf16[320,3584]{1,0:T(8,128)(2,1)} %broadcast_select_fusion.11), channel_id=9, source_target_pairs={{0,15},{1,0},{2,1},{3,2},{4,3},{5,4},{6,5},{7,6},{8,7},{9,8},{10,9... | collective-permute-start | bytes 6881288 | tf_op jit(solution)/dot_general | solution.py:14
  1051.3 33.0 %collective-permute-start.6 = (bf16[320,3584]{1,0:T(8,128)(2,1)}, bf16[320,3584]{1,0:T(8,128)(2,1)}, u32[]{:S(2)}, u32[]{:S(2)}) collective-permute-start(bf16[320,3584]{1,0:T(8,128)(2,1)} %get-tuple-element.160), channel_id=12, source_target_pairs={{0,1},{1,2},{2,3},{3,4},{4,5},{5,6},{6,7},{7,8},{8,9},{9,10},{10,1... | collective-permute-start | bytes 6881288 | tf_op jit(solution)/dot_general | solution.py:14
  1109.5 35.8 %collective-permute-start.4 = (bf16[320,3584]{1,0:T(8,128)(2,1)}, bf16[320,3584]{1,0:T(8,128)(2,1)}, u32[]{:S(2)}, u32[]{:S(2)}) collective-permute-start(bf16[320,3584]{1,0:T(8,128)(2,1)} %broadcast_select_fusion.10), channel_id=10, source_target_pairs={{0,1},{1,2},{2,3},{3,4},{4,5},{5,6},{6,7},{7,8},{8,9},{9,10},{10,1... | collective-permute-start | bytes 6881288 | tf_op jit(solution)/dot_general | solution.py:14
  1167.1 33.1 %collective-permute-start.6 = (bf16[320,3584]{1,0:T(8,128)(2,1)}, bf16[320,3584]{1,0:T(8,128)(2,1)}, u32[]{:S(2)}, u32[]{:S(2)}) collective-permute-start(bf16[320,3584]{1,0:T(8,128)(2,1)} %get-tuple-element.160), channel_id=12, source_target_pairs={{0,1},{1,2},{2,3},{3,4},{4,5},{5,6},{6,7},{7,8},{8,9},{9,10},{10,1... | collective-permute-start | bytes 6881288 | tf_op jit(solution)/dot_general | solution.py:14
  1222.0 173.4 %collective-permute-start.9 = (bf16[320,3584]{1,0:T(8,128)(2,1)}, bf16[320,3584]{1,0:T(8,128)(2,1)}, u32[]{:S(2)}, u32[]{:S(2)}) collective-permute-start(bf16[320,3584]{1,0:T(8,128)(2,1)} %get-tuple-element.15), channel_id=13, source_target_pairs={{0,1},{1,2},{2,3},{3,4},{4,5},{5,6},{6,7},{7,8},{8,9},{9,10},{10,1... | collective-permute-start | bytes 6881288 | tf_op jit(solution)/dot_general | solution.py:14
  (18 other events, 1026.2 us)
Sparse Core Ops, SparseCore 0:
  10.2 144.3 all-gather.6
  156.9 248.6 all-gather.8
where the time goes:
time: 1410 us
  starting transfers between devices  507 us (36%)
  waiting for transfers between devices  433 us (31%)
  matrix products  318 us (23%)
  other arithmetic  114 us (8%)
  local copies, waits for them, and re-layouts  19.9 us (1%)
  between operations  14.5 us (1%)
    dot_general x34, starting transfers between devices, step(): dx = jnp.dot(d_gate, w_gate.T) + jnp.dot(d_up, w_up.T)  507 us
    dot_general x34, waiting for transfers between devices, step(): dx = jnp.dot(d_gate, w_gate.T) + jnp.dot(d_up, w_up.T)  286 us
    unnamed x4, waiting for transfers between devices  147 us
    dot_general x16, matrix products, step(): dx = jnp.dot(d_gate, w_gate.T) + jnp.dot(d_up, w_up.T)  130 us
    dot_general x3, matrix products, by_group(): jnp.einsum('gta,gtb->gab', a, b, preferred_element_type=jnp.float32)  129 us
    dot_general x16, other arithmetic, step(): dx = jnp.dot(d_gate, w_gate.T) + jnp.dot(d_up, w_up.T)  74.8 us
    dot_general x1, matrix products, step(): d_hidden = jnp.dot(dy, w_down.T, preferred_element_type=jnp.float32)  58.1 us
    dot_general x16, other arithmetic  34.9 us
  transfers between devices with their start and end apart: 36, of which 18 were waited for; matrix products, arithmetic and copies ran while one was open for 32% of the time, Pallas kernels for 0%

commit v1 on v0

v1 whole, which is shorter than its diff:
```python
import jax
import jax.numpy as jnp
from jax.sharding import PartitionSpec as P


def act(gate, up):
    return jax.nn.gelu(gate) * up


def solution(mesh):
    def body(x, dy, gate, up, w_gate, w_up, w_down):
        dy_all = jax.lax.all_gather(dy, "tp", axis=0, tiled=True)
        x_all = jax.lax.all_gather(x, "tp", axis=0, tiled=True)
        hidden, back = jax.vjp(act, gate.astype(jnp.float32), up.astype(jnp.float32))
        d_hidden = jax.lax.dot_general(dy_all, w_down, (((1,), (1,)), ((), ())), preferred_element_type=jnp.float32)
        d_gate, d_up = (g.astype(jnp.bfloat16) for g in back(d_hidden))
        hidden = hidden.astype(jnp.bfloat16)
        dx = jax.lax.dot_general(d_gate, w_gate, (((1,), (1,)), ((), ())), preferred_element_type=jnp.float32)
        dx = dx + jax.lax.dot_general(d_up, w_up, (((1,), (1,)), ((), ())), preferred_element_type=jnp.float32)
        dx = jax.lax.psum_scatter(dx.astype(jnp.bfloat16), "tp", scatter_dimension=0, tiled=True)

        def over_tokens(a, b):
            product = jax.lax.dot_general(a, b, (((0,), (0,)), ((), ())), preferred_element_type=jnp.float32)
            return product.astype(jnp.bfloat16)

        return dx, over_tokens(x_all, d_gate), over_tokens(x_all, d_up), over_tokens(hidden, dy_all)

    rows, cols = P(("dp", "tp"), None), P("dp", "tp")
    return jax.shard_map(
        body,
        mesh=mesh,
        in_specs=(rows, rows, cols, cols, P(None, "tp"), P(None, "tp"), P("tp", None)),
        out_specs=(rows, cols, cols, rows),
        check_vma=False,
    )
```

time: 1410 us -> 696 us (0.49)
  starting transfers between devices: 507 us -> 0.11 us
  other arithmetic: 114 us -> 0 us
  waiting for transfers between devices: 433 us -> 364 us
  matrix products: 318 us -> 294 us
    dot_general x34 -> x0, starting transfers between devices: 507 us -> none  [step(): dx = jnp.dot(d_gate, w_gate.T) + jnp.dot(d_up, w_up.T)]
    dot_general x34 -> x0, waiting for transfers between devices: 286 us -> none  [step(): dx = jnp.dot(d_gate, w_gate.T) + jnp.dot(d_up, w_up.T)]
    reduce_scatter x0 -> x1, waiting for transfers between devices: none -> 217 us  [body(): jax.lax.psum_scatter(dx.astype(jnp.bfloat16), 'tp', scatter_dimension=0,...]
    all_gather x0 -> x2, waiting for transfers between devices: none -> 146 us  [the longest x1 146 us: body(): dy_all = jax.lax.all_gather(dy, 'tp', axis=0, tiled=True)]
    unnamed x4 -> x3, waiting for transfers between devices: 147 us -> 1.39 us
    dot_general x32 -> x0, other arithmetic: 110 us -> none  [the longest x16 74.8 us: step(): dx = jnp.dot(d_gate, w_gate.T) + jnp.dot(d_up, w_up.T)]
    dot_general x20 -> x6, matrix products: 318 us -> 294 us  [the longest x3 136 us: over_tokens(): jax.lax.dot_general(a, b, (((0,), (0,)), ((), ())), preferred_element_typ...]
  transfers between devices with their start and end apart: 36 -> 3, of which waited for: 18 -> 2; matrix products, arithmetic and copies ran while one was open for 32% -> 45% of each run, Pallas kernels for 0% -> 0%
where the time goes in v1:
time: 696 us; the launch traced here: 691 us
  waiting for transfers between devices  364 us (52%)
  matrix products  294 us (42%)
  local copies, waits for them, and re-layouts  19.1 us (3%)
  between operations  13.8 us (2%)
    reduce_scatter x1, waiting for transfers between devices, body(): jax.lax.psum_scatter(dx.astype(jnp.bfloat16), 'tp', scatter_dimension=0,...  217 us
    all_gather x1, waiting for transfers between devices, body(): dy_all = jax.lax.all_gather(dy, 'tp', axis=0, tiled=True)  146 us
    dot_general x3, matrix products, over_tokens(): jax.lax.dot_general(a, b, (((0,), (0,)), ((), ())), preferred_element_typ...  136 us
    dot_general x1, matrix products, body(): jax.lax.dot_general(dy_all, w_down, (((1,), (1,)), ((), ())), preferred_e...  56.9 us
    dot_general x1, matrix products, body(): jax.lax.dot_general(d_up, w_up, (((1,), (1,)), ((), ())), preferred_eleme...  54.2 us
    dot_general x1, matrix products, body(): jax.lax.dot_general(d_gate, w_gate, (((1,), (1,)), ((), ())), preferred_e...  47 us
    unnamed x2, local copies, waits for them, and re-layouts  19.1 us
  transfers between devices with their start and end apart: 3, of which 2 were waited for; matrix products, arithmetic and copies ran while one was open for 45% of the time, Pallas kernels for 0%

profile of v1, /device:TPU:0, one launch (start us, length us, event | category | flops | bytes accessed | tf_op | source)
XLA Modules:
  0.0 691.4 jit_solution(8858260944106497480)
XLA Ops:
  7.2 0.0 all-gather.3.cloned.1.call-start
  7.2 0.7 all-gather.3.cloned.1.call-update
  7.9 0.0 all-gather.5.cloned.1.call-start
  7.9 0.7 all-gather.5.cloned.1.call-update
  8.6 0.0 reduce-scatter.2.cloned.1.call-start
  8.7 145.9 %all-gather.3.cloned.1.call-done = bf16[5120,3584]{1,0:T(8,128)(2,1)} async-done(((bf16[320,3584]{1,0:T(8,128)(2,1)}), bf16[5120,3584]{1,0:T(8,128)(2,1)}) %all-gather.3.cloned.1.call-update) | async-done | bytes 36700176 | tf_op jit(solution)/shard_map/all_gather | solution.py:12
  154.6 56.9 %fusion.4 = (bf16[5120,896]{1,0:T(8,128)(2,1)}, f32[5120,896]{1,0:T(8,128)}) fusion(bf16[5120,896]{1,0:T(8,128)(2,1)} %param.9, bf16[5120,896]{1,0:T(8,128)(2,1)} %param.10, bf16[5120,3584]{1,0:T(8,128)(2,1)} %all-gather.3.cloned.1.call-done, bf16[896,3584]{1,0:T(8,128)(2,1)} %param.13), kind=kOutput, calls=%fused_computation.12 | convolution fusion | flops 32988856320 | bytes 88997888 | tf_op jit(solution)/shard_map/dot_general | solution.py:15
  211.5 47.0 %fusion.25 = f32[5120,3584]{1,0:T(8,128)} fusion(bf16[5120,896]{1,0:T(8,128)(2,1)} %get-tuple-element.8, bf16[3584,896]{1,0:T(8,128)(2,1)} %param.11), kind=kOutput, calls=%fused_computation.33 | convolution fusion | flops 32883343360 | bytes 88997888 | tf_op jit(solution)/shard_map/dot_general | solution.py:18
  258.6 54.2 %add_convert_fusion = bf16[5120,3584]{1,0:T(8,128)(2,1)} fusion(f32[5120,3584]{1,0:T(8,128)} %fusion.25, bf16[3584,896]{1,0:T(8,128)(2,1)} %param.12, f32[5120,896]{1,0:T(8,128)} %get-tuple-element.9, bf16[5120,896]{1,0:T(8,128)(2,1)} %param.9), kind=kOutput, calls=%fused_computation | convolution fusion | flops 32970506240 | bytes 144048128 | tf_op jit(solution)/shard_map/dot_general | solution.py:19
  312.8 0.0 reduce-scatter.2.cloned.1.call-update
  312.8 0.0 all-gather.5.cloned.1.call-done
  312.8 47.5 %fusion.20 = bf16[3584,896]{0,1:T(8,128)(2,1)} fusion(bf16[5120,3584]{1,0:T(8,128)(2,1)} %all-gather.5.cloned.1.call-done, f32[5120,896]{1,0:T(8,128)} %get-tuple-element.9, bf16[5120,896]{1,0:T(8,128)(2,1)} %param.9), kind=kOutput, calls=%fused_computation.28 | convolution fusion | flops 32937017344 | bytes 70647808 | tf_op jit(solution)/shard_map/dot_general | solution.py:23
  360.3 9.6 %copy.12 = bf16[3584,896]{1,0:T(8,128)(2,1)} copy(bf16[3584,896]{0,1:T(8,128)(2,1)} %fusion.20) | data formatting | bytes 12845056
  369.9 40.6 %fusion.19 = bf16[3584,896]{0,1:T(8,128)(2,1)} fusion(bf16[5120,896]{1,0:T(8,128)(2,1)} %get-tuple-element.8, bf16[5120,3584]{1,0:T(8,128)(2,1)} %all-gather.5.cloned.1.call-done), kind=kOutput, calls=%fused_computation.27 | convolution fusion | flops 32886554624 | bytes 52297728 | tf_op jit(solution)/shard_map/dot_general | solution.py:23
  410.5 9.6 %copy.11 = bf16[3584,896]{1,0:T(8,128)(2,1)} copy(bf16[3584,896]{0,1:T(8,128)(2,1)} %fusion.19) | data formatting | bytes 12845056
  420.1 47.7 %fusion.16 = bf16[896,3584]{1,0:T(8,128)(2,1)} fusion(bf16[5120,3584]{1,0:T(8,128)(2,1)} %all-gather.3.cloned.1.call-done, bf16[5120,896]{1,0:T(8,128)(2,1)} %param.10, bf16[5120,896]{1,0:T(8,128)(2,1)} %param.9), kind=kOutput, calls=%fused_computation.24 | convolution fusion | flops 32941604864 | bytes 61472768 | tf_op jit(solution)/shard_map/dot_general | solution.py:23
  467.8 217.0 %reduce-scatter.2.cloned.1.call-done = bf16[320,3584]{1,0:T(8,128)(2,1)} async-done(((bf16[5120,3584]{1,0:T(8,128)(2,1)}), bf16[320,3584]{1,0:T(8,128)(2,1)}) %reduce-scatter.2.cloned.1.call-update) | async-done | bytes 2293776 | tf_op jit(solution)/shard_map/reduce_scatter | solution.py:20
Async XLA Ops:
  7.2 147.5 %all-gather.3.cloned.1.call-start = ((), (), s32[]{:S(2)}) async-start(), calls=%async_computation.1 | async-start | bytes 38993920 | tf_op jit(solution)/shard_map/all_gather | solution.py:12
  7.9 304.9 %all-gather.5.cloned.1.call-start = ((), (), s32[]{:S(2)}) async-start(), calls=%async_computation.3 | async-start | bytes 38993920 | tf_op jit(solution)/shard_map/all_gather | solution.py:13
  8.6 676.2 %reduce-scatter.2.cloned.1.call-start = ((), (), s32[]{:S(2)}) async-start(), calls=%async_computation.2 | async-start | bytes 38993920 | tf_op jit(solution)/shard_map/reduce_scatter | solution.py:20
Sparse Core Ops, SparseCore 0:
  10.2 144.3 all-gather.2
  156.9 141.5 all-gather.4
  312.9 371.8 reduce-scatter.1

commit v2 on v1

v2 whole, which is shorter than its diff:
```python
import functools

import jax
import jax.numpy as jnp
from jax import lax
from jax.experimental import pallas as pl
from jax.experimental.pallas import tpu as pltpu
from jax.sharding import PartitionSpec as P

BF = jnp.bfloat16
F32 = jnp.float32
S = 10
R = 32
RING = 8
CHUNK = 16 * R
HALF = 8 * R
D = 3584
FL = 896
MASKS = (8, 4, 2)
BIT = (4, 2, 1)
HALVES = ((0, 1792), (1792, 1792))
THIRDS = ((0, 1152), (1152, 1280), (2432, 1152))
PAIRS = ((0, 1), (1, 2), (2, 0))
OTHERS = ((1, 2), (0, 2), (0, 1))
XYZ = 7
VMEM_LIMIT = 67_000_000


def act(gate, up):
    return jax.nn.gelu(gate) * up


def flip(me, mask):
    return me + mask * (1 - 2 * ((me // mask) % 2))


def peers_of(me):
    return [flip(me, m) for m in MASKS] + [flip(me, 1)]


def greet(peers):
    barrier = pltpu.get_barrier_semaphore()
    for peer in peers:
        pl.semaphore_signal(barrier, inc=1, device_id={"tp": peer}, device_id_type=pl.DeviceIdType.MESH)
    pl.semaphore_wait(barrier, len(peers))


def send(src, dst, send_sem, recv_sem, peer):
    return pltpu.make_async_remote_copy(
        src_ref=src, dst_ref=dst, send_sem=send_sem, recv_sem=recv_sem,
        device_id={"tp": peer}, device_id_type=pl.DeviceIdType.MESH,
    )


def gather_kernel(dy, x, gate, up, w_down, dgu, dw_gate, dw_up, dw_down, buf,
                  wd_v, acc, rows_v, gate_v, up_v, dgu_v, ht_v, stage,
                  ss, rs, load_sem, act_sem, w_sem, put_sem, out_sem):
    me = lax.axis_index("tp")
    peers = peers_of(me)
    last = 2 * S

    def place(g, v, core):
        return buf.at[g, pl.ds((core * 8 + v) * R, R)]

    def part(g, v, cols):
        return buf.at[g, pl.ds(v * R, R), pl.ds(*cols)]

    def own(g):
        return dy.at[pl.ds(g * R, R)], x.at[pl.ds((g - S) * R, R)]

    def copy(src, dst, g, k, peer):
        return send(src, dst, ss.at[g % RING, k], rs.at[g % RING, k], peer)

    def to_axis(g, d, src):
        return copy(src, place(g, BIT[d], 0), g, d, peers[d])

    def relay(g, q, h):
        a, b = PAIRS[q]
        via, src = (a, b) if h == 0 else (b, a)
        return copy(part(g, BIT[src], HALVES[h]), part(g, BIT[a] + BIT[b], HALVES[h]), g, 3 + 2 * q + h, peers[via])

    def relay_last(g, d):
        o, p = OTHERS[d]
        return copy(part(g, BIT[o] + BIT[p], THIRDS[d]), part(g, XYZ, THIRDS[d]), g, 9 + d, peers[d])

    def to_core(g, k, v, src=None):
        return copy(place(g, v, 0) if src is None else src, place(g, v, 1), g, 12 + k, peers[3])

    core_places = [0] + [BIT[d] for d in range(3)] + [BIT[a] + BIT[b] for a, b in PAIRS] + [XYZ]

    def stage0(g):
        @pl.when(g < S)
        def _():
            src, _ = own(g)
            for d in range(3):
                to_axis(g, d, src).start()
            to_core(g, 0, 0, src).start()

        @pl.when(g >= S)
        def _():
            _, src = own(g)
            for d in range(3):
                to_axis(g, d, src).start()
            to_core(g, 0, 0, src).start()

    def stage1(g):
        for d in range(3):
            to_axis(g, d, place(g, 0, 0)).wait_recv()
        for q in range(3):
            for h in range(2):
                relay(g, q, h).start()
        for d in range(3):
            to_core(g, 1 + d, BIT[d]).start()

    def stage2(g):
        for q in range(3):
            for h in range(2):
                relay(g, q, h).wait_recv()
        for d in range(3):
            relay_last(g, d).start()
        for q in range(3):
            to_core(g, 4 + q, core_places[4 + q]).start()

    def loads(g, slot):
        rest = pltpu.make_async_copy(buf.at[g, pl.ds(R, CHUNK - R)], rows_v.at[slot, pl.ds(R, CHUNK - R)], load_sem.at[slot, 0])
        mine = [pltpu.make_async_copy(src, rows_v.at[slot, pl.ds(0, R)], load_sem.at[slot, 1]) for src in own(g)]
        return rest, mine

    def act_loads(c, slot):
        for core in range(2):
            for v in range(8):
                j = me
                for d in range(3):
                    if v & BIT[d]:
                        j = flip(j, MASKS[d])
                if core:
                    j = flip(j, 1)
                at = pl.multiple_of(j * (S * R) + c * R, R)
                to = pl.ds((core * 8 + v) * R, R)
                pltpu.make_async_copy(gate.at[pl.ds(at, R)], gate_v.at[slot, to], act_sem.at[slot, 0]).start()
                pltpu.make_async_copy(up.at[pl.ds(at, R)], up_v.at[slot, to], act_sem.at[slot, 1]).start()

    def act_wait(slot):
        pltpu.make_async_copy(gate.at[pl.ds(0, CHUNK)], gate_v.at[slot], act_sem.at[slot, 0]).wait()
        pltpu.make_async_copy(up.at[pl.ds(0, CHUNK)], up_v.at[slot], act_sem.at[slot, 1]).wait()

    def dgu_load(c, slot):
        return pltpu.make_async_copy(dgu.at[c], dgu_v.at[slot], act_sem.at[slot, 0])

    def dgu_store(c, slot):
        return pltpu.make_async_copy(dgu_v.at[slot], dgu.at[c], put_sem.at[slot])

    def stage3(g):
        for d in range(3):
            relay_last(g, d).wait_recv()
        to_core(g, 7, XYZ).start()
        for k, v in enumerate(core_places):
            to_core(g, k, v).wait_recv()
        slot = g % 2
        rest, mine = loads(g, slot)
        rest.start()

        @pl.when(g < S)
        def _():
            mine[0].start()
            act_loads(g, slot)

        @pl.when(g >= S)
        def _():
            mine[1].start()

            @pl.when(g >= S + 2)
            def _():
                dgu_load(g - S, slot).start()

    def drain(g):
        for d in range(3):
            to_axis(g, d, place(g, 0, 0)).wait_send()
            relay_last(g, d).wait_send()
        for q in range(3):
            for h in range(2):
                relay(g, q, h).wait_send()
        for k, v in enumerate(core_places):
            to_core(g, k, v).wait_send()

    def act_tile(slot, t):
        rows = pl.ds(t * 256, 256)
        d_hidden = lax.dot_general(rows_v[slot, rows, :], wd_v[...], (((1,), (1,)), ((), ())), preferred_element_type=F32)
        hidden, back = jax.vjp(act, gate_v[slot, rows, :].astype(F32), up_v[slot, rows, :].astype(F32))
        d_gate, d_up = back(d_hidden)
        dgu_v[slot, rows, pl.ds(0, FL)] = d_gate.astype(BF)
        dgu_v[slot, rows, pl.ds(FL, FL)] = d_up.astype(BF)
        ht_v[:, rows] = hidden.T.astype(BF)

    def down_tile(slot, n):
        cols = pl.ds(pl.multiple_of(n * FL, 128), FL)
        rows, to = pl.ds(pl.multiple_of((n // 2) * FL, FL), FL), pl.ds(pl.multiple_of((n % 2) * FL, FL), FL)
        acc[rows, to] += jnp.dot(ht_v[...], rows_v[slot, :, cols], preferred_element_type=F32)

    def put_down():
        copies = []
        for i in range(14):
            r, c = i % 7, i // 7
            if i >= 2:
                copies[i - 2].wait()
            rows, cols = pl.ds(r * 128, 128), pl.ds(c * 1792, 1792)
            stage[i % 2, pl.ds(0, 128), :] = acc[pl.ds(i * 128, 128), :].astype(BF)
            copies.append(pltpu.make_async_copy(stage.at[i % 2, pl.ds(0, 128)], dw_down.at[rows, cols], out_sem.at[i % 2, 0]))
            copies[i].start()
        copies[12].wait()
        copies[13].wait()
        acc[pl.ds(0, 2 * FL), :] = jnp.zeros((2 * FL, 2 * FL), F32)

    def put_gu(m, slot):
        rows = pl.ds(pl.multiple_of(m * 256, 256), 256)
        return (
            pltpu.make_async_copy(stage.at[slot, :, pl.ds(0, FL)], dw_gate.at[rows], out_sem.at[slot, 0]),
            pltpu.make_async_copy(stage.at[slot, :, pl.ds(FL, FL)], dw_up.at[rows], out_sem.at[slot, 1]),
        )

    def gu_tile(g, slot, m):
        rows = pl.ds(pl.multiple_of(m * 256, 256), 256)
        acc[rows, :] += lax.dot_general(rows_v[slot, :, rows], dgu_v[slot], (((0,), (0,)), ((), ())), preferred_element_type=F32)

        @pl.when(g == last - 1)
        def _():
            at = m % 2

            @pl.when(m >= 2)
            def _():
                for c in put_gu(m - 2, at):
                    c.wait()

            stage[at] = acc[rows, :].astype(BF)
            for c in put_gu(m, at):
                c.start()

    def compute_first(g):
        slot = g % 2

        @pl.when(g < S)
        def _():
            rest, mine = loads(g, slot)
            rest.wait()
            mine[0].wait()
            act_wait(slot)

            @pl.when(g >= 2)
            def _():
                dgu_store(g - 2, slot).wait()

            act_tile(slot, 0)

        @pl.when(g >= S)
        def _():
            rest, mine = loads(g, slot)
            rest.wait()
            mine[1].wait()

            @pl.when(g < S + 2)
            def _():
                dgu_store(g - 2, slot).wait()
                dgu_load(g - S, slot).start()

            dgu_load(g - S, slot).wait()

            @pl.loop(0, 7)
            def _(m):
                gu_tile(g, slot, m)

    def compute_second(g):
        slot = g % 2

        @pl.when(g < S)
        def _():
            act_tile(slot, 1)
            dgu_store(g, slot).start()

            @pl.loop(0, 4)
            def _(n):
                down_tile(slot, n)

            @pl.when(g == S - 1)
            def _():
                put_down()

        @pl.when(g >= S)
        def _():
            @pl.loop(7, 14)
            def _(m):
                gu_tile(g, slot, m)

    weights = pltpu.make_async_copy(w_down, wd_v, w_sem)
    weights.start()
    greet(peers)
    stage0(jnp.int32(0))
    stage0(jnp.int32(1))
    acc[...] = jnp.zeros_like(acc)
    weights.wait()

    @pl.loop(0, last + 3)
    def _(i):
        @pl.when(i < last)
        def _():
            stage1(i)

        @pl.when(i + 2 < last)
        def _():
            @pl.when(i + 2 >= RING)
            def _():
                drain(i + 2 - RING)

            stage0(i + 2)

        @pl.when(i >= 3)
        def _():
            compute_first(i - 3)

        @pl.when(jnp.logical_and(i >= 1, i < last + 1))
        def _():
            stage2(i - 1)

        @pl.when(i >= 3)
        def _():
            compute_second(i - 3)

        @pl.when(jnp.logical_and(i >= 2, i < last + 2))
        def _():
            stage3(i - 2)

    @pl.loop(last - RING, last)
    def _(g):
        drain(g)

    for m in (12, 13):
        for c in put_gu(m, m % 2):
            c.wait()


def scatter_kernel(dgu, w_gate, w_up, dx,
                   w_v, dgu_v, part_v, core_s, core_r, s3, r3, s2, r2, s1, r1, out_v,
                   ss, rs, load_sem, w_sem, out_sem):
    me = lax.axis_index("tp")
    peers = peers_of(me)
    ring = 4

    def copy(src, dst, g, k, peer):
        return send(src, dst, ss.at[g % ring, k], rs.at[g % ring, k], peer)

    def to_core(g):
        return copy(core_s.at[g % 2], core_r.at[g % 2], g, 0, peers[3])

    def third(g, d):
        cols = pl.ds(*THIRDS[d])
        return copy(s3.at[g % 2, :, cols], r3.at[g % ring, :, cols], g, 1 + d, peers[d])

    def second(g, q, h):
        cols = pl.ds(*HALVES[h])
        return copy(s2.at[g % 2, q, :, cols], r2.at[g % ring, q, :, cols], g, 4 + 2 * q + h, peers[PAIRS[q][h]])

    def first(g, d):
        return copy(s1.at[g % 2, d], r1.at[g % ring, d], g, 10 + d, peers[d])

    def rows(v):
        return pl.ds(v * R, R)

    def load(g):
        return pltpu.make_async_copy(dgu.at[g], dgu_v.at[g % 2], load_sem.at[g % 2])

    def put(g):
        return pltpu.make_async_copy(out_v.at[g % 2], dx.at[pl.ds(pl.multiple_of(g * R, R), R)], out_sem.at[g % 2])

    def before(g, waits):
        @pl.when(g >= 2)
        def _():
            for c in waits(g - 2):
                c.wait_send()

    def thirds(g):
        return [third(g, d) for d in range(3)]

    def seconds(g):
        return [second(g, q, h) for q in range(3) for h in range(2)]

    def firsts(g):
        return [first(g, d) for d in range(3)]

    def multiply(g):
        slot = g % 2
        load(g).wait()

        @pl.when(g + 1 < S)
        def _():
            load(g + 1).start()

        before(g, lambda h: [to_core(h)])

        @pl.loop(0, 7)
        def _(n):
            cols = pl.ds(pl.multiple_of(n * 512, 512), 512)
            product = lax.dot_general(dgu_v[slot], w_v[cols, :], (((1,), (1,)), ((), ())), preferred_element_type=F32)
            part_v[g % 5, :, cols] = product[:HALF]
            core_s[slot, :, cols] = product[HALF:].astype(BF)

        to_core(g).start()

    def add_core(g):
        to_core(g).wait_recv()
        before(g, thirds)
        at = g % 5
        s3[g % 2] = (part_v[at, rows(XYZ), :] + core_r[g % 2, rows(XYZ), :].astype(F32)).astype(BF)
        low = pl.ds(0, XYZ * R)
        part_v[at, low, :] = part_v[at, low, :] + core_r[g % 2, low, :].astype(F32)
        for c in thirds(g):
            c.start()

    def add_thirds(g):
        for c in thirds(g):
            c.wait_recv()
        before(g, seconds)
        at = g % 5
        for q, (a, b) in enumerate(PAIRS):
            d = 3 - a - b
            v = BIT[a] + BIT[b]
            for e in range(3):
                cols = pl.ds(*THIRDS[e])
                value = part_v[at, rows(v), cols]
                if e == d:
                    value = value + r3[g % ring, :, cols].astype(F32)
                s2[g % 2, q, :, cols] = value.astype(BF)
        for c in seconds(g):
            c.start()

    def add_seconds(g):
        for c in seconds(g):
            c.wait_recv()
        before(g, firsts)
        at = g % 5
        for q, (a, b) in enumerate(PAIRS):
            for h, d in ((0, b), (1, a)):
                cols = pl.ds(*HALVES[h])
                s1[g % 2, d, :, cols] = (part_v[at, rows(BIT[d]), cols] + r2[g % ring, q, :, cols].astype(F32)).astype(BF)
        for c in firsts(g):
            c.start()

    def add_firsts(g):
        for c in firsts(g):
            c.wait_recv()

        @pl.when(g >= 2)
        def _():
            put(g - 2).wait()

        total = part_v[g % 5, rows(0), :]
        for d in range(3):
            total = total + r1[g % ring, d].astype(F32)
        out_v[g % 2] = total.astype(BF)
        put(g).start()

    w_copies = [
        pltpu.make_async_copy(w_gate, w_v.at[:, pl.ds(0, FL)], w_sem.at[0]),
        pltpu.make_async_copy(w_up, w_v.at[:, pl.ds(FL, FL)], w_sem.at[1]),
    ]
    for c in w_copies:
        c.start()
    load(jnp.int32(0)).start()
    greet(peers)
    for c in w_copies:
        c.wait()

    @pl.loop(0, S + 4)
    def _(i):
        for lag, step in ((2, add_thirds), (3, add_seconds), (4, add_firsts), (1, add_core)):
            @pl.when(jnp.logical_and(i >= lag, i < S + lag))
            def _(lag=lag, step=step):
                step(i - lag)

        @pl.when(i < S)
        def _():
            multiply(i)

    for g in (S - 2, S - 1):
        g = jnp.int32(g)
        for c in [to_core(g), *thirds(g), *seconds(g), *firsts(g)]:
            c.wait_send()
        put(g).wait()


def solution(mesh):
    any_space = pl.BlockSpec(memory_space=pl.ANY)
    dma = pltpu.SemaphoreType.DMA

    def body(x, dy, gate, up, w_gate, w_up, w_down):
        dgu, dw_gate, dw_up, dw_down, _ = pl.pallas_call(
            gather_kernel,
            out_shape=[
                jax.ShapeDtypeStruct((S, CHUNK, 2 * FL), BF),
                jax.ShapeDtypeStruct((D, FL), BF),
                jax.ShapeDtypeStruct((D, FL), BF),
                jax.ShapeDtypeStruct((FL, D), BF),
                jax.ShapeDtypeStruct((2 * S, CHUNK, D), BF),
            ],
            in_specs=[any_space] * 5,
            out_specs=[any_space] * 5,
            scratch_shapes=[
                pltpu.VMEM((FL, D), BF),
                pltpu.VMEM((D, 2 * FL), F32),
                pltpu.VMEM((2, CHUNK, D), BF),
                pltpu.VMEM((2, CHUNK, FL), BF),
                pltpu.VMEM((2, CHUNK, FL), BF),
                pltpu.VMEM((2, CHUNK, 2 * FL), BF),
                pltpu.VMEM((FL, CHUNK), BF),
                pltpu.VMEM((2, 256, 2 * FL), BF),
                dma((RING, 20)),
                dma((RING, 20)),
                dma((2, 2)),
                dma((2, 2)),
                dma,
                dma((2,)),
                dma((2, 2)),
            ],
            compiler_params=pltpu.CompilerParams(collective_id=0, has_side_effects=True, vmem_limit_bytes=VMEM_LIMIT),
            name="gather_dy_x",
        )(dy, x, gate, up, w_down)
        dx = pl.pallas_call(
            scatter_kernel,
            out_shape=jax.ShapeDtypeStruct((S * R, D), BF),
            in_specs=[any_space] * 3,
            out_specs=any_space,
            scratch_shapes=[
                pltpu.VMEM((D, 2 * FL), BF),
                pltpu.VMEM((2, CHUNK, 2 * FL), BF),
                pltpu.VMEM((5, HALF, D), F32),
                pltpu.VMEM((2, HALF, D), BF),
                pltpu.VMEM((2, HALF, D), BF),
                pltpu.VMEM((2, R, D), BF),
                pltpu.VMEM((4, R, D), BF),
                pltpu.VMEM((2, 3, R, D), BF),
                pltpu.VMEM((4, 3, R, D), BF),
                pltpu.VMEM((2, 3, R, D), BF),
                pltpu.VMEM((4, 3, R, D), BF),
                pltpu.VMEM((2, R, D), BF),
                dma((4, 13)),
                dma((4, 13)),
                dma((2,)),
                dma((2,)),
                dma((2,)),
            ],
            compiler_params=pltpu.CompilerParams(collective_id=1, has_side_effects=True, vmem_limit_bytes=VMEM_LIMIT),
            name="scatter_dx",
        )(dgu, w_gate, w_up)
        return dx, dw_gate, dw_up, dw_down

    rows, cols = P(("dp", "tp"), None), P("dp", "tp")
    return jax.shard_map(
        body,
        mesh=mesh,
        in_specs=(rows, rows, cols, cols, P(None, "tp"), P(None, "tp"), P("tp", None)),
        out_specs=(rows, cols, cols, rows),
        check_vma=False,
    )
```

time: 696 us -> 490 us (0.70)
  Pallas kernels: 0 us -> 473 us
  waiting for transfers between devices: 364 us -> 0 us
  matrix products: 294 us -> 0 us
  between operations: 13.8 us -> 0.67 us
    pallas_call x0 -> x2, Pallas kernels: none -> 473 us  [the longest x1 321 us: body(): pl.pallas_call(gather_kernel, out_shape=[jax.ShapeDtypeStruct((S, CHUNK,...]
    dot_general x6 -> x0, matrix products: 294 us -> none  [the longest x3 136 us: over_tokens(): jax.lax.dot_general(a, b, (((0,), (0,)), ((), ())), preferred_element_typ...]
    reduce_scatter x1 -> x0, waiting for transfers between devices: 217 us -> none  [body(): jax.lax.psum_scatter(dx.astype(jnp.bfloat16), 'tp', scatter_dimension=0,...]
    all_gather x2 -> x0, waiting for transfers between devices: 146 us -> none  [the longest x1 146 us: body(): dy_all = jax.lax.all_gather(dy, 'tp', axis=0, tiled=True)]
    unnamed x2 -> x12, local copies, waits for them, and re-layouts: 19.1 us -> 15.5 us
  transfers between devices with their start and end apart: 3 -> 0, of which waited for: 2 -> 0; matrix products, arithmetic and copies ran while one was open for 45% -> 0% of each run, Pallas kernels for 0% -> 0%
where the time goes in v2:
time: 490 us; the launch traced here: 489 us
  Pallas kernels  473 us (97%)
  local copies, waits for them, and re-layouts  15.5 us (3%)
    pallas_call x1, Pallas kernels, body(): pl.pallas_call(gather_kernel, out_shape=[jax.ShapeDtypeStruct((S, CHUNK,...  321 us
    pallas_call x1, Pallas kernels, body(): pl.pallas_call(scatter_kernel, out_shape=jax.ShapeDtypeStruct((S * R, D),...  152 us
    unnamed x12, local copies, waits for them, and re-layouts  15.5 us

profile of v2, /device:TPU:0, one launch (start us, length us, event | category | flops | bytes accessed | tf_op | source)
XLA Modules:
  0.0 489.4 jit_solution(17206075966360157910)
XLA Ops:
  0.6 321.1 %gather_dy_x.1 = (bf16[10,512,1792]{2,1,0:T(8,128)(2,1)}, bf16[3584,896]{1,0:T(8,128)(2,1)}, bf16[3584,896]{1,0:T(8,128)(2,1)}, bf16[896,3584]{1,0:T(8,128)(2,1)}, bf16[20,512,3584]{2,1,0:T(8,128)(2,1)}) custom-call(bf16[320,3584]{1,0:T(8,128)(2,1)} %dy.1, bf16[320,3584]{1,0:T(8,128)(2,1)} %x.1, bf16[5120,896]{1,0:T(8,128)(2,1)} %gate.1, ...), custom_call_target="tpu_custom_call" | custom-call | tf_op jit(solution)/shard_map/gather_dy_x/pallas_call | solution.py:494
  321.8 152.0 %scatter_dx.1 = bf16[320,3584]{1,0:T(8,128)(2,1)} custom-call(bf16[10,512,1792]{2,1,0:T(8,128)(2,1)} %get-tuple-element.8.dgu, bf16[3584,896]{1,0:T(8,128)(2,1)} %w_gate.1, bf16[3584,896]{1,0:T(8,128)(2,1)} %w_up.1), custom_call_target="tpu_custom_call" | custom-call | tf_op jit(solution)/shard_map/scatter_dx/pallas_call | solution.py:525
  473.8 0.0 slice-start.2
  473.8 3.3 copy.15
  477.1 0.0 slice-start.3
  477.1 0.0 slice-start
  477.1 6.2 %copy.16 = bf16[3584,896]{1,0:T(8,128)(2,1)} copy(bf16[3584,896]{1,0:T(8,128)(2,1)} %get-tuple-element.17) | data formatting | bytes 12845056
  483.4 0.0 slice-done.2
  483.4 0.0 slice-done.3
  483.4 0.0 slice-start.1
  483.4 2.9 copy.17
  486.3 0.0 slice-done
  486.3 0.3 slice-done.1
  486.6 2.7 copy.18
  (2 shorter events, 0.0 us)
Async XLA Ops:
  473.8 9.6 %slice-start.2 = ((s8[6422528]{0:T(1024)(128)(4,1)}), s8[4194304]{0:T(1024)(128)(4,1)S(1)}, s32[]{:S(2)}) async-start(s8[6422528]{0:T(1024)(128)(4,1)} %bitcast.2), calls=%async_computation.2 | async-start | bytes 8388608
  477.1 6.2 %slice-start.3 = ((s8[6422528]{0:T(1024)(128)(4,1)}), s8[2228224]{0:T(1024)(128)(4,1)S(1)}, s32[]{:S(2)}) async-start(s8[6422528]{0:T(1024)(128)(4,1)} %bitcast.2), calls=%async_computation.3 | async-start | bytes 4456448
  477.1 9.2 %slice-start = ((s8[6422528]{0:T(1024)(128)(4,1)}), s8[4194304]{0:T(1024)(128)(4,1)S(1)}, s32[]{:S(2)}) async-start(s8[6422528]{0:T(1024)(128)(4,1)} %bitcast), calls=%async_computation | async-start | bytes 8388608
  483.4 3.2 slice-start.1

commit v3 on v2

--- a/solution.py
+++ b/solution.py
@@ -23,6 +23,11 @@
 PAIRS = ((0, 1), (1, 2), (2, 0))
 OTHERS = ((1, 2), (0, 2), (0, 1))
 XYZ = 7
+TA = 512
+TM = 256
+NM = 8
+NB = D // TM - NM
+UG = 4
 VMEM_LIMIT = 67_000_000
 
 
@@ -184,7 +189,7 @@
             to_core(g, k, v).wait_send()
 
     def act_tile(slot, t):
-        rows = pl.ds(t * 256, 256)
+        rows = pl.ds(t * TA, TA)
         d_hidden = lax.dot_general(rows_v[slot, rows, :], wd_v[...], (((1,), (1,)), ((), ())), preferred_element_type=F32)
         hidden, back = jax.vjp(act, gate_v[slot, rows, :].astype(F32), up_v[slot, rows, :].astype(F32))
         d_gate, d_up = back(d_hidden)
@@ -212,28 +217,41 @@
         acc[pl.ds(0, 2 * FL), :] = jnp.zeros((2 * FL, 2 * FL), F32)
 
     def put_gu(m, slot):
-        rows = pl.ds(pl.multiple_of(m * 256, 256), 256)
+        rows = pl.ds(pl.multiple_of(m * TM, TM), TM)
         return (
             pltpu.make_async_copy(stage.at[slot, :, pl.ds(0, FL)], dw_gate.at[rows], out_sem.at[slot, 0]),
             pltpu.make_async_copy(stage.at[slot, :, pl.ds(FL, FL)], dw_up.at[rows], out_sem.at[slot, 1]),
         )
 
-    def gu_tile(g, slot, m):
-        rows = pl.ds(pl.multiple_of(m * 256, 256), 256)
-        acc[rows, :] += lax.dot_general(rows_v[slot, :, rows], dgu_v[slot], (((0,), (0,)), ((), ())), preferred_element_type=F32)
+    def gu_tile(slot, m, flush):
+        rows = pl.ds(pl.multiple_of(m * TM, TM), TM)
+        total = acc[rows, :] + lax.dot_general(rows_v[slot, :, rows], dgu_v[slot], (((0,), (0,)), ((), ())), preferred_element_type=F32)
+        if not flush:
+            acc[rows, :] = total
+            return
+        at = m % 2
+
+        @pl.when(m >= 2)
+        def _():
+            for c in put_gu(m - 2, at):
+                c.wait()
+
+        stage[at] = total.astype(BF)
+        for c in put_gu(m, at):
+            c.start()
+
+    def gu_tiles(g, slot, low, high):
+        @pl.when(g < last - 1)
+        def _():
+            @pl.loop(low, high, unroll=UG)
+            def _(m):
+                gu_tile(slot, m, False)
 
         @pl.when(g == last - 1)
         def _():
-            at = m % 2
-
-            @pl.when(m >= 2)
-            def _():
-                for c in put_gu(m - 2, at):
-                    c.wait()
-
-            stage[at] = acc[rows, :].astype(BF)
-            for c in put_gu(m, at):
-                c.start()
+            @pl.loop(low, high)
+            def _(m):
+                gu_tile(slot, m, True)
 
     def compute_first(g):
         slot = g % 2
@@ -249,7 +267,8 @@
             def _():
                 dgu_store(g - 2, slot).wait()
 
-            act_tile(slot, 0)
+            for t in range(CHUNK // TA // 2 + CHUNK // TA % 2):
+                act_tile(slot, t)
 
         @pl.when(g >= S)
         def _():
@@ -264,16 +283,15 @@
 
             dgu_load(g - S, slot).wait()
 
-            @pl.loop(0, 7)
-            def _(m):
-                gu_tile(g, slot, m)
+            gu_tiles(g, slot, 0, NM // 2)
 
     def compute_second(g):
         slot = g % 2
 
         @pl.when(g < S)
         def _():
-            act_tile(slot, 1)
+            for t in range(CHUNK // TA // 2 + CHUNK // TA % 2, CHUNK // TA):
+                act_tile(slot, t)
             dgu_store(g, slot).start()
 
             @pl.loop(0, 4)
@@ -286,9 +304,7 @@
 
         @pl.when(g >= S)
         def _():
-            @pl.loop(7, 14)
-            def _(m):
-                gu_tile(g, slot, m)
+            gu_tiles(g, slot, NM // 2, NM)
 
     weights = pltpu.make_async_copy(w_down, wd_v, w_sem)
     weights.start()
@@ -298,7 +314,7 @@
     acc[...] = jnp.zeros_like(acc)
     weights.wait()
 
-    @pl.loop(0, last + 3)
+    @pl.loop(0, last + 4)
     def _(i):
         @pl.when(i < last)
         def _():
@@ -312,37 +328,38 @@
 
             stage0(i + 2)
 
-        @pl.when(i >= 3)
-        def _():
-            compute_first(i - 3)
+        @pl.when(jnp.logical_and(i >= 3, i < last + 3))
+        def _():
+            stage3(i - 3)
+
+        @pl.when(i >= 4)
+        def _():
+            compute_first(i - 4)
 
         @pl.when(jnp.logical_and(i >= 1, i < last + 1))
         def _():
             stage2(i - 1)
 
-        @pl.when(i >= 3)
-        def _():
-            compute_second(i - 3)
-
-        @pl.when(jnp.logical_and(i >= 2, i < last + 2))
-        def _():
-            stage3(i - 2)
+        @pl.when(i >= 4)
+        def _():
+            compute_second(i - 4)
 
     @pl.loop(last - RING, last)
     def _(g):
         drain(g)
 
-    for m in (12, 13):
+    for m in (NM - 2, NM - 1):
         for c in put_gu(m, m % 2):
             c.wait()
 
 
-def scatter_kernel(dgu, w_gate, w_up, dx,
-                   w_v, dgu_v, part_v, core_s, core_r, s3, r3, s2, r2, s1, r1, out_v,
-                   ss, rs, load_sem, w_sem, out_sem):
+def scatter_kernel(dgu, w_gate, w_up, x, buf, dw_gate_in, dw_up_in, dx, dw_gate, dw_up,
+                   acc, x_v, w_v, dgu_v, part_v, sum2, sum1, sum0, core_s, core_r, s3, r3, s2, r2, s1, r1, out_v,
+                   ss, rs, load_sem, x_sem, w_sem, out_sem, put_sem):
     me = lax.axis_index("tp")
     peers = peers_of(me)
     ring = 4
+    x_cols = pl.ds(NM * TM, NB * TM)
 
     def copy(src, dst, g, k, peer):
         return send(src, dst, ss.at[g % ring, k], rs.at[g % ring, k], peer)
@@ -365,7 +382,19 @@
         return pl.ds(v * R, R)
 
     def load(g):
-        return pltpu.make_async_copy(dgu.at[g], dgu_v.at[g % 2], load_sem.at[g % 2])
+        at = g % 2
+        return (
+            pltpu.make_async_copy(dgu.at[g], dgu_v.at[at], load_sem.at[at]),
+            pltpu.make_async_copy(x.at[pl.ds(pl.multiple_of(g * R, R), R), x_cols], x_v.at[at, pl.ds(0, R)], x_sem.at[at, 0]),
+            pltpu.make_async_copy(buf.at[S + g, pl.ds(R, CHUNK - R), x_cols], x_v.at[at, pl.ds(R, CHUNK - R)], x_sem.at[at, 1]),
+        )
+
+    def put_gu(m):
+        rows, src = pl.ds((NM + m) * TM, TM), w_v.at[pl.ds(m * TM, TM)]
+        return (
+            pltpu.make_async_copy(src.at[:, pl.ds(0, FL)], dw_gate.at[rows], put_sem.at[m, 0]),
+            pltpu.make_async_copy(src.at[:, pl.ds(FL, FL)], dw_up.at[rows], put_sem.at[m, 1]),
+        )
 
     def put(g):
         return pltpu.make_async_copy(out_v.at[g % 2], dx.at[pl.ds(pl.multiple_of(g * R, R), R)], out_sem.at[g % 2])
@@ -387,30 +416,41 @@
 
     def multiply(g):
         slot = g % 2
-        load(g).wait()
+        for c in load(g):
+            c.wait()
 
         @pl.when(g + 1 < S)
         def _():
-            load(g + 1).start()
+            for c in load(g + 1):
+                c.start()
 
         before(g, lambda h: [to_core(h)])
 
-        @pl.loop(0, 7)
+        @pl.loop(0, 7, unroll=7)
         def _(n):
             cols = pl.ds(pl.multiple_of(n * 512, 512), 512)
             product = lax.dot_general(dgu_v[slot], w_v[cols, :], (((1,), (1,)), ((), ())), preferred_element_type=F32)
-            part_v[g % 5, :, cols] = product[:HALF]
+            part_v[:, cols] = product[:HALF]
             core_s[slot, :, cols] = product[HALF:].astype(BF)
 
         to_core(g).start()
+        for m in range(NB):
+            rows = pl.ds(m * TM, TM)
+            acc[rows, :] += lax.dot_general(x_v[slot, :, rows], dgu_v[slot], (((0,), (0,)), ((), ())), preferred_element_type=F32)
 
     def add_core(g):
         to_core(g).wait_recv()
         before(g, thirds)
-        at = g % 5
-        s3[g % 2] = (part_v[at, rows(XYZ), :] + core_r[g % 2, rows(XYZ), :].astype(F32)).astype(BF)
-        low = pl.ds(0, XYZ * R)
-        part_v[at, low, :] = part_v[at, low, :] + core_r[g % 2, low, :].astype(F32)
+
+        def both(v):
+            return part_v[rows(v), :] + core_r[g % 2, rows(v), :].astype(F32)
+
+        s3[g % 2] = both(XYZ).astype(BF)
+        for q, (a, b) in enumerate(PAIRS):
+            sum2[g % 2, q] = both(BIT[a] + BIT[b])
+        for d in range(3):
+            sum1[g % 3, d] = both(BIT[d])
+        sum0[g % 4] = both(0)
         for c in thirds(g):
             c.start()
 
@@ -418,13 +458,11 @@
         for c in thirds(g):
             c.wait_recv()
         before(g, seconds)
-        at = g % 5
         for q, (a, b) in enumerate(PAIRS):
             d = 3 - a - b
-            v = BIT[a] + BIT[b]
             for e in range(3):
                 cols = pl.ds(*THIRDS[e])
-                value = part_v[at, rows(v), cols]
+                value = sum2[g % 2, q, :, cols]
                 if e == d:
                     value = value + r3[g % ring, :, cols].astype(F32)
                 s2[g % 2, q, :, cols] = value.astype(BF)
@@ -435,11 +473,10 @@
         for c in seconds(g):
             c.wait_recv()
         before(g, firsts)
-        at = g % 5
         for q, (a, b) in enumerate(PAIRS):
             for h, d in ((0, b), (1, a)):
                 cols = pl.ds(*HALVES[h])
-                s1[g % 2, d, :, cols] = (part_v[at, rows(BIT[d]), cols] + r2[g % ring, q, :, cols].astype(F32)).astype(BF)
+                s1[g % 2, d, :, cols] = (sum1[g % 3, d, :, cols] + r2[g % ring, q, :, cols].astype(F32)).astype(BF)
         for c in firsts(g):
             c.start()
 
@@ -451,7 +488,7 @@
         def _():
             put(g - 2).wait()
 
-        total = part_v[g % 5, rows(0), :]
+        total = sum0[g % 4]
         for d in range(3):
             total = total + r1[g % ring, d].astype(F32)
         out_v[g % 2] = total.astype(BF)
@@ -463,14 +500,16 @@
     ]
     for c in w_copies:
         c.start()
-    load(jnp.int32(0)).start()
+    for c in load(jnp.int32(0)):
+        c.start()
     greet(peers)
+    acc[...] = jnp.zeros_like(acc)
     for c in w_copies:
         c.wait()
 
     @pl.loop(0, S + 4)
     def _(i):
-        for lag, step in ((2, add_thirds), (3, add_seconds), (4, add_firsts), (1, add_core)):
+        for lag, step in ((1, add_core), (2, add_thirds), (3, add_seconds), (4, add_firsts)):
             @pl.when(jnp.logical_and(i >= lag, i < S + lag))
             def _(lag=lag, step=step):
                 step(i - lag)
@@ -478,12 +517,23 @@
         @pl.when(i < S)
         def _():
             multiply(i)
+
+        @pl.when(i == S)
+        def _():
+            for m in range(NB):
+                w_v[pl.ds(m * TM, TM), :] = acc[pl.ds(m * TM, TM), :].astype(BF)
+            for m in range(NB):
+                for c in put_gu(m):
+                    c.start()
 
     for g in (S - 2, S - 1):
         g = jnp.int32(g)
         for c in [to_core(g), *thirds(g), *seconds(g), *firsts(g)]:
             c.wait_send()
         put(g).wait()
+    for m in range(NB):
+        for c in put_gu(m):
+            c.wait()
 
 
 def solution(mesh):
@@ -491,7 +541,7 @@
     dma = pltpu.SemaphoreType.DMA
 
     def body(x, dy, gate, up, w_gate, w_up, w_down):
-        dgu, dw_gate, dw_up, dw_down, _ = pl.pallas_call(
+        dgu, dw_gate, dw_up, dw_down, buf = pl.pallas_call(
             gather_kernel,
             out_shape=[
                 jax.ShapeDtypeStruct((S, CHUNK, 2 * FL), BF),
@@ -504,13 +554,13 @@
             out_specs=[any_space] * 5,
             scratch_shapes=[
                 pltpu.VMEM((FL, D), BF),
-                pltpu.VMEM((D, 2 * FL), F32),
+                pltpu.VMEM((NM * TM, 2 * FL), F32),
                 pltpu.VMEM((2, CHUNK, D), BF),
                 pltpu.VMEM((2, CHUNK, FL), BF),
                 pltpu.VMEM((2, CHUNK, FL), BF),
                 pltpu.VMEM((2, CHUNK, 2 * FL), BF),
                 pltpu.VMEM((FL, CHUNK), BF),
-                pltpu.VMEM((2, 256, 2 * FL), BF),
+                pltpu.VMEM((2, TM, 2 * FL), BF),
                 dma((RING, 20)),
                 dma((RING, 20)),
                 dma((2, 2)),
@@ -522,15 +572,25 @@
             compiler_params=pltpu.CompilerParams(collective_id=0, has_side_effects=True, vmem_limit_bytes=VMEM_LIMIT),
             name="gather_dy_x",
         )(dy, x, gate, up, w_down)
-        dx = pl.pallas_call(
+        dx, dw_gate, dw_up = pl.pallas_call(
             scatter_kernel,
-            out_shape=jax.ShapeDtypeStruct((S * R, D), BF),
-            in_specs=[any_space] * 3,
-            out_specs=any_space,
+            out_shape=[
+                jax.ShapeDtypeStruct((S * R, D), BF),
+                jax.ShapeDtypeStruct((D, FL), BF),
+                jax.ShapeDtypeStruct((D, FL), BF),
+            ],
+            in_specs=[any_space] * 7,
+            input_output_aliases={5: 1, 6: 2},
+            out_specs=[any_space] * 3,
             scratch_shapes=[
+                pltpu.VMEM((NB * TM, 2 * FL), F32),
+                pltpu.VMEM((2, CHUNK, NB * TM), BF),
                 pltpu.VMEM((D, 2 * FL), BF),
                 pltpu.VMEM((2, CHUNK, 2 * FL), BF),
-                pltpu.VMEM((5, HALF, D), F32),
+                pltpu.VMEM((HALF, D), F32),
+                pltpu.VMEM((2, 3, R, D), F32),
+                pltpu.VMEM((3, 3, R, D), F32),
+                pltpu.VMEM((4, R, D), F32),
                 pltpu.VMEM((2, HALF, D), BF),
                 pltpu.VMEM((2, HALF, D), BF),
                 pltpu.VMEM((2, R, D), BF),
@@ -543,12 +603,14 @@
                 dma((4, 13)),
                 dma((4, 13)),
                 dma((2,)),
+                dma((2, 2)),
                 dma((2,)),
                 dma((2,)),
+                dma((NB, 2)),
             ],
             compiler_params=pltpu.CompilerParams(collective_id=1, has_side_effects=True, vmem_limit_bytes=VMEM_LIMIT),
             name="scatter_dx",
-        )(dgu, w_gate, w_up)
+        )(dgu, w_gate, w_up, x, buf, dw_gate, dw_up)
         return dx, dw_gate, dw_up, dw_down
 
     rows, cols = P(("dp", "tp"), None), P("dp", "tp")

time: 490 us -> 433 us (0.88)
  Pallas kernels: 473 us -> 416 us
    pallas_call x1, Pallas kernels: 321 us -> 263 us  [body(): pl.pallas_call(gather_kernel, out_shape=[jax.ShapeDtypeStruct((S, CHUNK,...]
where the time goes in v3:
time: 433 us
  Pallas kernels  416 us (96%)
  local copies, waits for them, and re-layouts  15.5 us (4%)
    pallas_call x1, Pallas kernels, body(): pl.pallas_call(gather_kernel, out_shape=[jax.ShapeDtypeStruct((S, CHUNK,...  263 us
    pallas_call x1, Pallas kernels, body(): pl.pallas_call(scatter_kernel, out_shape=[jax.ShapeDtypeStruct((S * R, D)...  154 us
    unnamed x12, local copies, waits for them, and re-layouts  15.5 us

profile of v3, /device:TPU:0, one launch (start us, length us, event | category | flops | bytes accessed | tf_op | source)
XLA Modules:
  0.0 432.7 jit_solution(1927031271831878208)
XLA Ops:
  0.6 262.7 %gather_dy_x.1 = (bf16[10,512,1792]{2,1,0:T(8,128)(2,1)}, bf16[3584,896]{1,0:T(8,128)(2,1)}, bf16[3584,896]{1,0:T(8,128)(2,1)}, bf16[896,3584]{1,0:T(8,128)(2,1)}, bf16[20,512,3584]{2,1,0:T(8,128)(2,1)}) custom-call(bf16[320,3584]{1,0:T(8,128)(2,1)} %dy.1, bf16[320,3584]{1,0:T(8,128)(2,1)} %x.3, bf16[5120,896]{1,0:T(8,128)(2,1)} %gate.1, ...), custom_call_target="tpu_custom_call" | custom-call | tf_op jit(solution)/shard_map/gather_dy_x/pallas_call | solution.py:544
  263.4 153.7 %scatter_dx.1 = (bf16[320,3584]{1,0:T(8,128)(2,1)}, bf16[3584,896]{1,0:T(8,128)(2,1)}, bf16[3584,896]{1,0:T(8,128)(2,1)}) custom-call(bf16[10,512,1792]{2,1,0:T(8,128)(2,1)} %get-tuple-element.12.dgu, bf16[3584,896]{1,0:T(8,128)(2,1)} %w_gate.1, bf16[3584,896]{1,0:T(8,128)(2,1)} %w_up.1, ...), custom_call_target="tpu_custom_call", output_to_operand_aliasing={{1}: (5, {}), {2}: (6, {})} | custom-call | tf_op jit(solution)/shard_map/scatter_dx/pallas_call | solution.py:575
  417.1 0.0 slice-start
  417.1 3.3 copy.19
  420.5 0.0 slice-start.1
  420.5 0.0 slice-start.2
  420.5 6.2 %copy.20 = bf16[3584,896]{1,0:T(8,128)(2,1)} copy(bf16[3584,896]{1,0:T(8,128)(2,1)} %get-tuple-element.25) | data formatting | bytes 12845056
  426.7 0.0 slice-done
  426.7 0.0 slice-done.1
  426.7 0.0 slice-start.3
  426.7 2.9 copy.21
  429.6 0.0 slice-done.2
  429.6 0.3 slice-done.3
  429.9 2.7 copy.22
  (2 shorter events, 0.0 us)
Async XLA Ops:
  417.1 9.6 %slice-start = ((s8[6422528]{0:T(1024)(128)(4,1)}), s8[4194304]{0:T(1024)(128)(4,1)S(1)}, s32[]{:S(2)}) async-start(s8[6422528]{0:T(1024)(128)(4,1)} %bitcast), calls=%async_computation | async-start | bytes 8388608
  420.5 6.2 %slice-start.1 = ((s8[6422528]{0:T(1024)(128)(4,1)}), s8[2228224]{0:T(1024)(128)(4,1)S(1)}, s32[]{:S(2)}) async-start(s8[6422528]{0:T(1024)(128)(4,1)} %bitcast), calls=%async_computation.1 | async-start | bytes 4456448
  420.5 9.2 %slice-start.2 = ((s8[6422528]{0:T(1024)(128)(4,1)}), s8[4194304]{0:T(1024)(128)(4,1)S(1)}, s32[]{:S(2)}) async-start(s8[6422528]{0:T(1024)(128)(4,1)} %bitcast.2), calls=%async_computation.2 | async-start | bytes 8388608
  426.7 3.2 slice-start.3

commit v4 on v3

--- a/solution.py
+++ b/solution.py
@@ -28,6 +28,10 @@
 NM = 8
 NB = D // TM - NM
 UG = 4
+LAG = 3
+X_STEPS = (((0, 0), (0, 1)), ((0, 2), (1, 0), (1, 1)), ((1, 2), (2, 0)), ((2, 1), (2, 2)))
+FT = 512
+XD = 3
 VMEM_LIMIT = 67_000_000
 
 
@@ -57,74 +61,92 @@
     )
 
 
-def gather_kernel(dy, x, gate, up, w_down, dgu, dw_gate, dw_up, dw_down, buf,
+def gather_ops(buf, ss, rs, ring, peers):
+    places = [0] + [BIT[d] for d in range(3)] + [BIT[a] + BIT[b] for a, b in PAIRS] + [XYZ]
+
+    def place(g, v, core):
+        return buf.at[g, pl.ds((core * 8 + v) * R, R)]
+
+    def part(g, v, cols):
+        return buf.at[g, pl.ds(v * R, R), pl.ds(*cols)]
+
+    def copy(src, dst, g, k, peer):
+        return send(src, dst, ss.at[g % ring, k], rs.at[g % ring, k], peer)
+
+    def to_axis(g, d, src=None):
+        return copy(place(g, 0, 0) if src is None else src, place(g, BIT[d], 0), g, d, peers[d])
+
+    def relays(g):
+        for q, (a, b) in enumerate(PAIRS):
+            for h, via, src in ((0, a, b), (1, b, a)):
+                yield copy(part(g, BIT[src], HALVES[h]), part(g, BIT[a] + BIT[b], HALVES[h]), g, 3 + 2 * q + h, peers[via])
+
+    def relay_last(g, d):
+        o, p = OTHERS[d]
+        return copy(part(g, BIT[o] + BIT[p], THIRDS[d]), part(g, XYZ, THIRDS[d]), g, 9 + d, peers[d])
+
+    def to_core(g, k, src=None):
+        return copy(place(g, places[k], 0) if src is None else src, place(g, places[k], 1), g, 12 + k, peers[3])
+
+    def start(g, src):
+        for d in range(3):
+            to_axis(g, d, src).start()
+        to_core(g, 0, src).start()
+
+    def stage1(g):
+        for d in range(3):
+            to_axis(g, d).wait_recv()
+        for c in relays(g):
+            c.start()
+        for k in (1, 2, 3):
+            to_core(g, k).start()
+
+    def stage2(g):
+        for c in relays(g):
+            c.wait_recv()
+        for d in range(3):
+            relay_last(g, d).start()
+        for k in (4, 5, 6):
+            to_core(g, k).start()
+
+    def arrive(g):
+        for d in range(3):
+            relay_last(g, d).wait_recv()
+        to_core(g, 7).start()
+        for k in range(8):
+            to_core(g, k).wait_recv()
+
+    def drain(g):
+        for d in range(3):
+            to_axis(g, d).wait_send()
+            relay_last(g, d).wait_send()
+        for c in relays(g):
+            c.wait_send()
+        for k in range(8):
+            to_core(g, k).wait_send()
+
+    return start, stage1, stage2, arrive, drain
+
+
+def gather_kernel(dy, x, gate, up, w_down, dgu, dw_part, dw_down, buf,
                   wd_v, acc, rows_v, gate_v, up_v, dgu_v, ht_v, stage,
                   ss, rs, load_sem, act_sem, w_sem, put_sem, out_sem):
     me = lax.axis_index("tp")
     peers = peers_of(me)
-    last = 2 * S
-
-    def place(g, v, core):
-        return buf.at[g, pl.ds((core * 8 + v) * R, R)]
-
-    def part(g, v, cols):
-        return buf.at[g, pl.ds(v * R, R), pl.ds(*cols)]
+    last = 2 * S - XD
+    start, stage1, stage2, arrive, drain = gather_ops(buf, ss, rs, RING, peers)
 
     def own(g):
         return dy.at[pl.ds(g * R, R)], x.at[pl.ds((g - S) * R, R)]
 
-    def copy(src, dst, g, k, peer):
-        return send(src, dst, ss.at[g % RING, k], rs.at[g % RING, k], peer)
-
-    def to_axis(g, d, src):
-        return copy(src, place(g, BIT[d], 0), g, d, peers[d])
-
-    def relay(g, q, h):
-        a, b = PAIRS[q]
-        via, src = (a, b) if h == 0 else (b, a)
-        return copy(part(g, BIT[src], HALVES[h]), part(g, BIT[a] + BIT[b], HALVES[h]), g, 3 + 2 * q + h, peers[via])
-
-    def relay_last(g, d):
-        o, p = OTHERS[d]
-        return copy(part(g, BIT[o] + BIT[p], THIRDS[d]), part(g, XYZ, THIRDS[d]), g, 9 + d, peers[d])
-
-    def to_core(g, k, v, src=None):
-        return copy(place(g, v, 0) if src is None else src, place(g, v, 1), g, 12 + k, peers[3])
-
-    core_places = [0] + [BIT[d] for d in range(3)] + [BIT[a] + BIT[b] for a, b in PAIRS] + [XYZ]
-
     def stage0(g):
         @pl.when(g < S)
         def _():
-            src, _ = own(g)
-            for d in range(3):
-                to_axis(g, d, src).start()
-            to_core(g, 0, 0, src).start()
+            start(g, own(g)[0])
 
         @pl.when(g >= S)
         def _():
-            _, src = own(g)
-            for d in range(3):
-                to_axis(g, d, src).start()
-            to_core(g, 0, 0, src).start()
-
-    def stage1(g):
-        for d in range(3):
-            to_axis(g, d, place(g, 0, 0)).wait_recv()
-        for q in range(3):
-            for h in range(2):
-                relay(g, q, h).start()
-        for d in range(3):
-            to_core(g, 1 + d, BIT[d]).start()
-
-    def stage2(g):
-        for q in range(3):
-            for h in range(2):
-                relay(g, q, h).wait_recv()
-        for d in range(3):
-            relay_last(g, d).start()
-        for q in range(3):
-            to_core(g, 4 + q, core_places[4 + q]).start()
+            start(g, own(g)[1])
 
     def loads(g, slot):
         rest = pltpu.make_async_copy(buf.at[g, pl.ds(R, CHUNK - R)], rows_v.at[slot, pl.ds(R, CHUNK - R)], load_sem.at[slot, 0])
@@ -156,11 +178,7 @@
         return pltpu.make_async_copy(dgu_v.at[slot], dgu.at[c], put_sem.at[slot])
 
     def stage3(g):
-        for d in range(3):
-            relay_last(g, d).wait_recv()
-        to_core(g, 7, XYZ).start()
-        for k, v in enumerate(core_places):
-            to_core(g, k, v).wait_recv()
+        arrive(g)
         slot = g % 2
         rest, mine = loads(g, slot)
         rest.start()
@@ -177,16 +195,6 @@
             @pl.when(g >= S + 2)
             def _():
                 dgu_load(g - S, slot).start()
-
-    def drain(g):
-        for d in range(3):
-            to_axis(g, d, place(g, 0, 0)).wait_send()
-            relay_last(g, d).wait_send()
-        for q in range(3):
-            for h in range(2):
-                relay(g, q, h).wait_send()
-        for k, v in enumerate(core_places):
-            to_core(g, k, v).wait_send()
 
     def act_tile(slot, t):
         rows = pl.ds(t * TA, TA)
@@ -216,42 +224,22 @@
         copies[13].wait()
         acc[pl.ds(0, 2 * FL), :] = jnp.zeros((2 * FL, 2 * FL), F32)
 
-    def put_gu(m, slot):
+    def put_gu(half):
+        rows = pl.ds(half * (NM // 2 * TM), NM // 2 * TM)
+        return pltpu.make_async_copy(acc.at[rows], dw_part.at[rows], out_sem.at[half, 1])
+
+    def gu_tile(slot, m):
         rows = pl.ds(pl.multiple_of(m * TM, TM), TM)
-        return (
-            pltpu.make_async_copy(stage.at[slot, :, pl.ds(0, FL)], dw_gate.at[rows], out_sem.at[slot, 0]),
-            pltpu.make_async_copy(stage.at[slot, :, pl.ds(FL, FL)], dw_up.at[rows], out_sem.at[slot, 1]),
-        )
-
-    def gu_tile(slot, m, flush):
-        rows = pl.ds(pl.multiple_of(m * TM, TM), TM)
-        total = acc[rows, :] + lax.dot_general(rows_v[slot, :, rows], dgu_v[slot], (((0,), (0,)), ((), ())), preferred_element_type=F32)
-        if not flush:
-            acc[rows, :] = total
-            return
-        at = m % 2
-
-        @pl.when(m >= 2)
-        def _():
-            for c in put_gu(m - 2, at):
-                c.wait()
-
-        stage[at] = total.astype(BF)
-        for c in put_gu(m, at):
-            c.start()
-
-    def gu_tiles(g, slot, low, high):
-        @pl.when(g < last - 1)
-        def _():
-            @pl.loop(low, high, unroll=UG)
-            def _(m):
-                gu_tile(slot, m, False)
+        acc[rows, :] += lax.dot_general(rows_v[slot, :, rows], dgu_v[slot], (((0,), (0,)), ((), ())), preferred_element_type=F32)
+
+    def gu_tiles(g, slot, half):
+        @pl.loop(half * (NM // 2), (half + 1) * (NM // 2), unroll=UG)
+        def _(m):
+            gu_tile(slot, m)
 
         @pl.when(g == last - 1)
         def _():
-            @pl.loop(low, high)
-            def _(m):
-                gu_tile(slot, m, True)
+            put_gu(half).start()
 
     def compute_first(g):
         slot = g % 2
@@ -283,7 +271,7 @@
 
             dgu_load(g - S, slot).wait()
 
-            gu_tiles(g, slot, 0, NM // 2)
+            gu_tiles(g, slot, 0)
 
     def compute_second(g):
         slot = g % 2
@@ -304,7 +292,7 @@
 
         @pl.when(g >= S)
         def _():
-            gu_tiles(g, slot, NM // 2, NM)
+            gu_tiles(g, slot, 1)
 
     weights = pltpu.make_async_copy(w_down, wd_v, w_sem)
     weights.start()
@@ -348,17 +336,17 @@
     def _(g):
         drain(g)
 
-    for m in (NM - 2, NM - 1):
-        for c in put_gu(m, m % 2):
-            c.wait()
-
-
-def scatter_kernel(dgu, w_gate, w_up, x, buf, dw_gate_in, dw_up_in, dx, dw_gate, dw_up,
-                   acc, x_v, w_v, dgu_v, part_v, sum2, sum1, sum0, core_s, core_r, s3, r3, s2, r2, s1, r1, out_v,
-                   ss, rs, load_sem, x_sem, w_sem, out_sem, put_sem):
+    for half in range(2):
+        put_gu(half).wait()
+
+
+def scatter_kernel(dgu, w_gate, w_up, x, buf, dw_part_in, dx, dw_part, buf_x,
+                   acc, x_v, dgu_x, w_v, dgu_v, part_v, sum2, sum1, sum0, core_s, core_r, s3, r3, s2, r2, s1, r1, out_v,
+                   ss, rs, xss, xrs, load_sem, x_sem, w_sem, out_sem, put_sem, own_sem):
     me = lax.axis_index("tp")
     peers = peers_of(me)
     ring = 4
+    start_x, stage1_x, stage2_x, arrive_x, drain_x = gather_ops(buf_x, xss, xrs, XD, peers)
     x_cols = pl.ds(NM * TM, NB * TM)
 
     def copy(src, dst, g, k, peer):
@@ -382,19 +370,45 @@
         return pl.ds(v * R, R)
 
     def load(g):
-        at = g % 2
+        return pltpu.make_async_copy(dgu.at[g], dgu_v.at[g % 2], load_sem.at[g % 2])
+
+    def rest_of_x(src):
+        return pltpu.make_async_copy(src.at[pl.ds(R, CHUNK - R), x_cols], x_v.at[pl.ds(R, CHUNK - R)], x_sem.at[2])
+
+    def load_gu(g):
         return (
-            pltpu.make_async_copy(dgu.at[g], dgu_v.at[at], load_sem.at[at]),
-            pltpu.make_async_copy(x.at[pl.ds(pl.multiple_of(g * R, R), R), x_cols], x_v.at[at, pl.ds(0, R)], x_sem.at[at, 0]),
-            pltpu.make_async_copy(buf.at[S + g, pl.ds(R, CHUNK - R), x_cols], x_v.at[at, pl.ds(R, CHUNK - R)], x_sem.at[at, 1]),
+            pltpu.make_async_copy(dgu.at[g], dgu_x, x_sem.at[0]),
+            pltpu.make_async_copy(x.at[pl.ds(pl.multiple_of(g * R, R), R), x_cols], x_v.at[pl.ds(0, R)], x_sem.at[1]),
         )
 
-    def put_gu(m):
-        rows, src = pl.ds((NM + m) * TM, TM), w_v.at[pl.ds(m * TM, TM)]
-        return (
-            pltpu.make_async_copy(src.at[:, pl.ds(0, FL)], dw_gate.at[rows], put_sem.at[m, 0]),
-            pltpu.make_async_copy(src.at[:, pl.ds(FL, FL)], dw_up.at[rows], put_sem.at[m, 1]),
-        )
+    def start_gu(g):
+        for c in load_gu(g):
+            c.start()
+
+        @pl.when(g < S - XD)
+        def _():
+            rest_of_x(buf.at[S + g]).start()
+
+        @pl.when(g >= S - XD)
+        def _():
+            rest_of_x(buf_x.at[g - (S - XD)]).start()
+
+    def add_gu(g):
+        for c in load_gu(g):
+            c.wait()
+        rest_of_x(buf_x.at[0]).wait()
+        for m in range(NB):
+            rows = pl.ds(m * TM, TM)
+            acc[rows, :] += lax.dot_general(x_v[:, rows], dgu_x[...], (((0,), (0,)), ((), ())), preferred_element_type=F32)
+
+    def put_gu():
+        return pltpu.make_async_copy(acc, dw_part.at[pl.ds(NM * TM, NB * TM)], put_sem)
+
+    def x_own(h):
+        return x.at[pl.ds((S - XD + h) * R, R)]
+
+    def keep_own(h):
+        return pltpu.make_async_copy(x_own(h), buf_x.at[h, pl.ds(0, R)], own_sem.at[h])
 
     def put(g):
         return pltpu.make_async_copy(out_v.at[g % 2], dx.at[pl.ds(pl.multiple_of(g * R, R), R)], out_sem.at[g % 2])
@@ -416,13 +430,11 @@
 
     def multiply(g):
         slot = g % 2
-        for c in load(g):
-            c.wait()
+        load(g).wait()
 
         @pl.when(g + 1 < S)
         def _():
-            for c in load(g + 1):
-                c.start()
+            load(g + 1).start()
 
         before(g, lambda h: [to_core(h)])
 
@@ -434,9 +446,6 @@
             core_s[slot, :, cols] = product[HALF:].astype(BF)
 
         to_core(g).start()
-        for m in range(NB):
-            rows = pl.ds(m * TM, TM)
-            acc[rows, :] += lax.dot_general(x_v[slot, :, rows], dgu_v[slot], (((0,), (0,)), ((), ())), preferred_element_type=F32)
 
     def add_core(g):
         to_core(g).wait_recv()
@@ -500,15 +509,23 @@
     ]
     for c in w_copies:
         c.start()
-    for c in load(jnp.int32(0)):
-        c.start()
+    load(jnp.int32(0)).start()
     greet(peers)
+    for h in range(XD):
+        start_x(h, x_own(h))
+        keep_own(h).start()
     acc[...] = jnp.zeros_like(acc)
     for c in w_copies:
         c.wait()
 
     @pl.loop(0, S + 4)
     def _(i):
+        gu_round = jnp.logical_and(i >= LAG, i < S + LAG)
+
+        @pl.when(gu_round)
+        def _():
+            start_gu(i - LAG)
+
         for lag, step in ((1, add_core), (2, add_thirds), (3, add_seconds), (4, add_firsts)):
             @pl.when(jnp.logical_and(i >= lag, i < S + lag))
             def _(lag=lag, step=step):
@@ -518,22 +535,50 @@
         def _():
             multiply(i)
 
-        @pl.when(i == S)
-        def _():
-            for m in range(NB):
-                w_v[pl.ds(m * TM, TM), :] = acc[pl.ds(m * TM, TM), :].astype(BF)
-            for m in range(NB):
-                for c in put_gu(m):
-                    c.start()
+        @pl.when(gu_round)
+        def _():
+            add_gu(i - LAG)
+
+        @pl.when(i == S + LAG - 1)
+        def _():
+            put_gu().start()
+
+        for at, steps in enumerate(X_STEPS):
+            @pl.when(i == at)
+            def _(steps=steps):
+                for step, h in steps:
+                    (stage1_x, stage2_x, arrive_x)[step](h)
 
     for g in (S - 2, S - 1):
         g = jnp.int32(g)
         for c in [to_core(g), *thirds(g), *seconds(g), *firsts(g)]:
             c.wait_send()
         put(g).wait()
-    for m in range(NB):
-        for c in put_gu(m):
-            c.wait()
+    put_gu().wait()
+    for h in range(XD):
+        drain_x(h)
+        keep_own(h).wait()
+
+
+def finish_kernel(part, dx_in, dw_down_in, *refs):
+    xs, dgus, (dx, dw_gate, dw_up, dw_down) = refs[:XD], refs[XD : 2 * XD], refs[2 * XD :]
+    dx[...] = dx_in[...]
+    dw_down[...] = dw_down_in[...]
+
+    def put(total):
+        dw_gate[...] = total[:, :FL].astype(BF)
+        dw_up[...] = total[:, FL:].astype(BF)
+
+    @pl.when(pl.program_id(0) * FT < NM * TM)
+    def _():
+        total = part[...]
+        for a, b in zip(xs, dgus):
+            total = total + lax.dot_general(a[...], b[...], (((0,), (0,)), ((), ())), preferred_element_type=F32)
+        put(total)
+
+    @pl.when(pl.program_id(0) * FT >= NM * TM)
+    def _():
+        put(part[...])
 
 
 def solution(mesh):
@@ -541,17 +586,16 @@
     dma = pltpu.SemaphoreType.DMA
 
     def body(x, dy, gate, up, w_gate, w_up, w_down):
-        dgu, dw_gate, dw_up, dw_down, buf = pl.pallas_call(
+        dgu, dw_part, dw_down, buf = pl.pallas_call(
             gather_kernel,
             out_shape=[
                 jax.ShapeDtypeStruct((S, CHUNK, 2 * FL), BF),
-                jax.ShapeDtypeStruct((D, FL), BF),
-                jax.ShapeDtypeStruct((D, FL), BF),
+                jax.ShapeDtypeStruct((D, 2 * FL), F32),
                 jax.ShapeDtypeStruct((FL, D), BF),
-                jax.ShapeDtypeStruct((2 * S, CHUNK, D), BF),
+                jax.ShapeDtypeStruct((2 * S - XD, CHUNK, D), BF),
             ],
             in_specs=[any_space] * 5,
-            out_specs=[any_space] * 5,
+            out_specs=[any_space] * 4,
             scratch_shapes=[
                 pltpu.VMEM((FL, D), BF),
                 pltpu.VMEM((NM * TM, 2 * FL), F32),
@@ -572,19 +616,20 @@
             compiler_params=pltpu.CompilerParams(collective_id=0, has_side_effects=True, vmem_limit_bytes=VMEM_LIMIT),
             name="gather_dy_x",
         )(dy, x, gate, up, w_down)
-        dx, dw_gate, dw_up = pl.pallas_call(
+        dx, dw_part, buf_x = pl.pallas_call(
             scatter_kernel,
             out_shape=[
                 jax.ShapeDtypeStruct((S * R, D), BF),
-                jax.ShapeDtypeStruct((D, FL), BF),
-                jax.ShapeDtypeStruct((D, FL), BF),
+                jax.ShapeDtypeStruct((D, 2 * FL), F32),
+                jax.ShapeDtypeStruct((XD, CHUNK, D), BF),
             ],
-            in_specs=[any_space] * 7,
-            input_output_aliases={5: 1, 6: 2},
+            in_specs=[any_space] * 6,
+            input_output_aliases={5: 1},
             out_specs=[any_space] * 3,
             scratch_shapes=[
                 pltpu.VMEM((NB * TM, 2 * FL), F32),
-                pltpu.VMEM((2, CHUNK, NB * TM), BF),
+                pltpu.VMEM((CHUNK, NB * TM), BF),
+                pltpu.VMEM((CHUNK, 2 * FL), BF),
                 pltpu.VMEM((D, 2 * FL), BF),
                 pltpu.VMEM((2, CHUNK, 2 * FL), BF),
                 pltpu.VMEM((HALF, D), F32),
@@ -602,15 +647,37 @@
                 pltpu.VMEM((2, R, D), BF),
                 dma((4, 13)),
                 dma((4, 13)),
+                dma((XD, 20)),
+                dma((XD, 20)),
                 dma((2,)),
-                dma((2, 2)),
+                dma((3,)),
                 dma((2,)),
                 dma((2,)),
-                dma((NB, 2)),
+                dma,
+                dma((XD,)),
             ],
             compiler_params=pltpu.CompilerParams(collective_id=1, has_side_effects=True, vmem_limit_bytes=VMEM_LIMIT),
             name="scatter_dx",
-        )(dgu, w_gate, w_up, x, buf, dw_gate, dw_up)
+        )(dgu, w_gate, w_up, x, buf, dw_part)
+        by_rows, x_cols = pl.BlockSpec((FT, FL), lambda m: (m, 0)), FT
+        dx_spec = pl.BlockSpec((S * R, x_cols), lambda m: (0, m))
+        down_spec = pl.BlockSpec((FL, x_cols), lambda m: (0, m))
+        dx, dw_gate, dw_up, dw_down = pl.pallas_call(
+            finish_kernel,
+            grid=(D // FT,),
+            out_shape=[
+                jax.ShapeDtypeStruct((S * R, D), BF),
+                jax.ShapeDtypeStruct((D, FL), BF),
+                jax.ShapeDtypeStruct((D, FL), BF),
+                jax.ShapeDtypeStruct((FL, D), BF),
+            ],
+            in_specs=[pl.BlockSpec((FT, 2 * FL), lambda m: (m, 0)), dx_spec, down_spec]
+            + [pl.BlockSpec((None, CHUNK, FT), lambda m, h=h: (h, 0, jnp.minimum(m, NM * TM // FT - 1))) for h in range(XD)]
+            + [pl.BlockSpec((None, CHUNK, 2 * FL), lambda m, h=h: (S - XD + h, 0, 0)) for h in range(XD)],
+            out_specs=[dx_spec, by_rows, by_rows, down_spec],
+            compiler_params=pltpu.CompilerParams(vmem_limit_bytes=VMEM_LIMIT),
+            name="finish_dw",
+        )(dw_part, dx, dw_down, *[buf_x] * XD, *[dgu] * XD)
         return dx, dw_gate, dw_up, dw_down
 
     rows, cols = P(("dp", "tp"), None), P("dp", "tp")

time: 433 us -> 423 us (0.977)
  local copies, waits for them, and re-layouts: 15.5 us -> 0 us
  Pallas kernels: 416 us -> 422 us
    pallas_call x1, Pallas kernels: 263 us -> 232 us  [body(): pl.pallas_call(gather_kernel, out_shape=[jax.ShapeDtypeStruct((S, CHUNK,...]
    pallas_call x0 -> x1, Pallas kernels: none -> 26.8 us  [body(): pl.pallas_call(finish_kernel, grid=(D // FT,), out_shape=[jax.ShapeDtypeS...]
    unnamed x12 -> x0, local copies, waits for them, and re-layouts: 15.5 us -> none
    pallas_call x1, Pallas kernels: 154 us -> 163 us  [body(): pl.pallas_call(scatter_kernel, out_shape=[jax.ShapeDtypeStruct((S * R, D)...]
where the time goes in v4:
time: 423 us
  Pallas kernels  422 us (100%)
    pallas_call x1, Pallas kernels, body(): pl.pallas_call(gather_kernel, out_shape=[jax.ShapeDtypeStruct((S, CHUNK,...  232 us
    pallas_call x1, Pallas kernels, body(): pl.pallas_call(scatter_kernel, out_shape=[jax.ShapeDtypeStruct((S * R, D)...  163 us
    pallas_call x1, Pallas kernels, body(): pl.pallas_call(finish_kernel, grid=(D // FT,), out_shape=[jax.ShapeDtypeS...  26.8 us

profile of v4, /device:TPU:0, one launch (start us, length us, event | category | flops | bytes accessed | tf_op | source)
XLA Modules:
  0.0 422.9 jit_solution(7104024538137809898)
XLA Ops:
  0.6 231.9 %gather_dy_x.1 = (bf16[10,512,1792]{2,1,0:T(8,128)(2,1)}, f32[3584,1792]{1,0:T(8,128)}, bf16[896,3584]{1,0:T(8,128)(2,1)}, bf16[17,512,3584]{2,1,0:T(8,128)(2,1)}) custom-call(bf16[320,3584]{1,0:T(8,128)(2,1)} %dy.1, bf16[320,3584]{1,0:T(8,128)(2,1)} %x.3, bf16[5120,896]{1,0:T(8,128)(2,1)} %gate.1, bf16[5120,896]{1,0:T(8,128)(2,1)} %up.1, ...), custom_call_target="tpu_custom_call" | custom-call | tf_op jit(solution)/shard_map/gather_dy_x/pallas_call | solution.py:589
  232.6 163.5 %scatter_dx.1 = (bf16[320,3584]{1,0:T(8,128)(2,1)}, f32[3584,1792]{1,0:T(8,128)}, bf16[3,512,3584]{2,1,0:T(8,128)(2,1)}) custom-call(bf16[10,512,1792]{2,1,0:T(8,128)(2,1)} %get-tuple-element.11.dgu.refs_3_.refs_4_.refs_5_, bf16[3584,896]{1,0:T(8,128)(2,1)} %w_gate.1, bf16[3584,896]{1,0:T(8,128)(2,1)} %w_up.1, ...), custom_call_target="tpu_custom_call", output_to_operand_aliasing={{1}: (5, {})} | custom-call | tf_op jit(solution)/shard_map/scatter_dx/pallas_call | solution.py:619
  396.1 26.8 %finish_dw.1 = (bf16[320,3584]{1,0:T(8,128)(2,1)}, bf16[3584,896]{1,0:T(8,128)(2,1)}, bf16[3584,896]{1,0:T(8,128)(2,1)}, bf16[896,3584]{1,0:T(8,128)(2,1)}) custom-call(f32[3584,1792]{1,0:T(8,128)} %get-tuple-element.14.part, bf16[320,3584]{1,0:T(8,128)(2,1)} %get-tuple-element.15.dx_in, bf16[896,3584]{1,0:T(8,128)(2,1)} %get-tuple-element.16.dw_down_in, ...), custom_call_target="tpu_custom_call" | custom-call | tf_op jit(solution)/shard_map/finish_dw/pallas_call | solution.py:665
